TPU v7x, 32 devices: a whole 2x2x4 slice. The times are simulated.
32 devices in a mesh: dp: 8 (over y, x, core), fsdp: 4 (over z).
Axes of the slice: x: 2, y: 2, z: 4, core: 2. Of those that a mesh axis runs over, the one named last changes fastest.
Arguments:
- latents: bfloat16 [2, 32, 4, 1024], P(None, ('dp', 'fsdp')), may hold values from -6 to 6
- noise: bfloat16 [2, 32, 4, 1024], P(None, ('dp', 'fsdp')), may hold values from -6 to 6
- context: bfloat16 [2, 32, 77, 768], P(None, ('dp', 'fsdp')), may hold values from -6 to 6
- timesteps: int32 [2, 32], P(None, ('dp', 'fsdp')), may hold values from 0 to 999
- region_mask: int32 [2, 32, 1024], P(None, ('dp', 'fsdp')), may hold values from 0 to 1, as said below
- owners: int32 [8], replicated, may hold values from 0 to 7, each once
- step_count: int32 [1], replicated, may hold values from 2 to 20
- kernels_weight: float32 [2, 2880, 320], P(None, 'dp', 'fsdp'), may hold values from -0.109375 to 0.109375
- kernels_first: float32 [2, 2880, 320], P(None, 'dp', 'fsdp'), may hold values from -6.4818124e-07 to 6.4818124e-07
- kernels_second: float32 [2, 2880, 320], P(None, 'dp', 'fsdp'), may hold values from 2.1701389e-15 to 8.6805554e-15
- entry_weight: float32 [320, 1280], P('dp', 'fsdp'), may hold values from -0.3125 to 0.3125
- entry_first: float32 [320, 1280], P('dp', 'fsdp'), may hold values from -6.875e-08 to 6.875e-08
- entry_second: float32 [320, 1280], P('dp', 'fsdp'), may hold values from 2.4414062e-17 to 9.765625e-17
- middle_weight: float32 [1280, 1280], P('dp', 'fsdp'), may hold values from -0.15625 to 0.15625
- middle_first: float32 [1280, 1280], P('dp', 'fsdp'), may hold values from -4.8125e-08 to 4.8125e-08
- middle_second: float32 [1280, 1280], P('dp', 'fsdp'), may hold values from 1.196289e-17 to 4.785156e-17
- narrow_weight: float32 [2, 1280, 320], P(None, 'dp', 'fsdp'), may hold values from -0.15625 to 0.15625
- narrow_first: float32 [2, 1280, 320], P(None, 'dp', 'fsdp'), may hold values from -1.1667262e-07 to 1.1667262e-07
- narrow_second: float32 [2, 1280, 320], P(None, 'dp', 'fsdp'), may hold values from 7.03125e-17 to 2.8125e-16
- crossing_weight: float32 [768, 640], P('dp', 'fsdp'), may hold values from -0.21875 to 0.21875
- crossing_first: float32 [768, 640], P('dp', 'fsdp'), may hold values from -4.518711e-08 to 4.518711e-08
- crossing_second: float32 [768, 640], P('dp', 'fsdp'), may hold values from 1.0546875e-17 to 4.21875e-17
- widen_weight: float32 [320, 2560], P('dp', 'fsdp'), may hold values from -0.3125 to 0.3125
- widen_first: float32 [320, 2560], P('dp', 'fsdp'), may hold values from -3.0140427e-08 to 3.0140427e-08
- widen_second: float32 [320, 2560], P('dp', 'fsdp'), may hold values from 4.6923826e-18 to 1.876953e-17
- vectors_weight: float32 [112, 320], P('dp', 'fsdp'), as said below
- vectors_first: float32 [112, 320], P('dp', 'fsdp'), may hold values from -4.6483483e-06 to 4.6483483e-06
- vectors_second: float32 [112, 320], P('dp', 'fsdp'), may hold values from 1.1160714e-13 to 4.4642857e-13
- squares_weight: float32 [8, 320, 320], P(None, 'dp', 'fsdp')
- squares_state: float32 [6, 8, 320, 320], P(None, 'fsdp'), as said below
Outputs:
- totals: float32 [2], replicated
- kernels_master: float32 [2, 2880, 320], P(None, 'dp', 'fsdp')
- kernels_moment: float32 [2, 2880, 320], P(None, 'dp', 'fsdp')
- kernels_variance: float32 [2, 2880, 320], P(None, 'dp', 'fsdp')
- entry_master: float32 [320, 1280], P('dp', 'fsdp')
- entry_moment: float32 [320, 1280], P('dp', 'fsdp')
- entry_variance: float32 [320, 1280], P('dp', 'fsdp')
- middle_master: float32 [1280, 1280], P('dp', 'fsdp')
- middle_moment: float32 [1280, 1280], P('dp', 'fsdp')
- middle_variance: float32 [1280, 1280], P('dp', 'fsdp')
- narrow_master: float32 [2, 1280, 320], P(None, 'dp', 'fsdp')
- narrow_moment: float32 [2, 1280, 320], P(None, 'dp', 'fsdp')
- narrow_variance: float32 [2, 1280, 320], P(None, 'dp', 'fsdp')
- crossing_master: float32 [768, 640], P('dp', 'fsdp')
- crossing_moment: float32 [768, 640], P('dp', 'fsdp')
- crossing_variance: float32 [768, 640], P('dp', 'fsdp')
- widen_master: float32 [320, 2560], P('dp', 'fsdp')
- widen_moment: float32 [320, 2560], P('dp', 'fsdp')
- widen_variance: float32 [320, 2560], P('dp', 'fsdp')
- vectors_master: float32 [112, 320], P('dp', 'fsdp')
- vectors_moment: float32 [112, 320], P('dp', 'fsdp')
- vectors_variance: float32 [112, 320], P('dp', 'fsdp')
- squares_master: float32 [8, 320, 320], P(None, 'dp', 'fsdp')
- squares_slots: float32 [2, 8, 320, 320], P(None, 'fsdp')
- squares_grad: float32 [8, 320, 320], P('fsdp')
Inputs may be any that keep to these rules, and one draw needn't show every extreme that they name: `region_mask`: 1 marks a pixel whose error counts; pixel 0 of every sample counts. `owners`: each slot names a different matrix; slot j is kept by the devices whose fsdp index is j // (8 // the number of fsdp devices). `vectors_weight`: rows as the steps name them. `squares_state`: in every slot the statistics L and R are symmetric positive definite and the bases QL and QR orthogonal.
All inputs are finite; a program needn't handle non-finite values.
Results may differ from a plain program's by a relative error of at most 0.012.
The roundings to bfloat16 on the way count: a program that leaves them out, or rounds other values in their place, can miss the bound.
Values may be sent and summed in bfloat16 or wider, within the bound.
A program may use at most 320 MiB of HBM per device.

v0:
```python
from functools import partial
import math

import jax
import jax.numpy as jnp
from jax import lax
from jax.sharding import PartitionSpec as P

C = 320
HEADS = 8
GROUPS = 32
CTX_DIM = 768
SIDE = 32
HEAD_DIM = 40


highest = lax.Precision.HIGHEST
beta_one = 0.9
beta_two = 0.999
beta_stat = 0.95
adam_eps = 1e-08
decay = 0.01
clip_limit = 0.002


def lowered(values):
    return values.astype(jnp.bfloat16)


def product(left_matrix, right_matrix):
    return jnp.dot(left_matrix, right_matrix, preferred_element_type=jnp.float32)


def product_left(left_matrix, right_matrix):
    return lax.dot_general(
        left_matrix, right_matrix, (((0,), (0,)), ((), ())), preferred_element_type=jnp.float32
    )


def product_right(left_matrix, right_matrix):
    return lax.dot_general(
        left_matrix, right_matrix, (((1,), (1,)), ((), ())), preferred_element_type=jnp.float32
    )


def column_sum(values):
    return jnp.sum(values.astype(jnp.float32), axis=0)


def rates():
    return (
        3.0 / math.sqrt(9 * C),
        3.0 / math.sqrt(C),
        3.0 / math.sqrt(4 * C),
        3.0 / math.sqrt(4 * C),
        3.0 / math.sqrt(CTX_DIM),
        3.0 / math.sqrt(C),
        0.3,
        3.0 / math.sqrt(C),
    )


def noise_level(timestep):
    levels = jnp.arange(1000, dtype=jnp.float32)
    roots = 0.00085**0.5 + (0.012**0.5 - 0.00085**0.5) * levels / 999.0
    signals = jnp.exp(jnp.cumsum(jnp.log1p(-roots * roots)))
    return jnp.sum(jnp.where(jnp.arange(1000) == timestep, signals, 0.0))


def time_features(timestep, channels):
    halfway = channels // 2
    freqs = jnp.exp(-math.log(10000.0) * jnp.arange(halfway, dtype=jnp.float32) / halfway)
    angles = timestep.astype(jnp.float32) * freqs
    return jnp.concatenate([jnp.cos(angles), jnp.sin(angles)])[None, :]


def group_norm(values, gain, offset, epsilon):
    pixels, channels = values.shape
    grouped = values.reshape(pixels, GROUPS, channels // GROUPS)
    average = jnp.mean(grouped, axis=(0, 2), keepdims=True)
    spread = jnp.mean(jnp.square(grouped - average), axis=(0, 2), keepdims=True)
    normal = ((grouped - average) * lax.rsqrt(spread + epsilon)).reshape(pixels, channels)
    return normal * gain + offset


def norm_silu(values, gain, offset, epsilon):
    return jax.nn.silu(group_norm(values, gain, offset, epsilon))


def layer_norm(values, gain, offset):
    average = jnp.mean(values, axis=1, keepdims=True)
    spread = jnp.mean(jnp.square(values - average), axis=1, keepdims=True)
    return (values - average) * lax.rsqrt(spread + 1e-05) * gain + offset


def geglu(gated):
    halfway = gated.shape[1] // 2
    return gated[:, :halfway] * jax.nn.gelu(gated[:, halfway:], approximate=False)


def unpack(vector_table):
    return dict(
        input_bias=vector_table[72],
        norm_one=vector_table[73:75],
        block_one_bias=vector_table[75],
        time_in_bias=vector_table[76:80].reshape(-1),
        middle_bias=vector_table[80:84].reshape(-1),
        time_out_bias=vector_table[84],
        norm_two=vector_table[85:87],
        block_two_bias=vector_table[87],
        norm_three=vector_table[88:90],
        project_in_bias=vector_table[90],
        layer_one=vector_table[91:93],
        self_bias=vector_table[93],
        layer_two=vector_table[94:96],
        cross_bias=vector_table[96],
        layer_three=vector_table[97:99],
        gate_bias=vector_table[99:107].reshape(-1),
        down_bias=vector_table[107],
        project_out_bias=vector_table[108],
        norm_out=vector_table[109:111],
        output_bias=vector_table[111, 0:4],
    )


def neighbours(image):
    channels = image.shape[1]
    padded = jnp.pad(image.reshape(SIDE, SIDE, channels), ((1, 1), (1, 1), (0, 0)))
    return jnp.concatenate(
        [
            padded[row_offset : row_offset + SIDE, col_offset : col_offset + SIDE].reshape(
                SIDE * SIDE, channels
            )
            for row_offset in range(3)
            for col_offset in range(3)
        ],
        axis=1,
    )


def fold_back(columns, channels):
    folded = jnp.zeros((SIDE + 2, SIDE + 2, channels), jnp.float32)
    for tap_index in range(9):
        row_offset, col_offset = (tap_index // 3, tap_index % 3)
        piece = columns[:, tap_index * channels : (tap_index + 1) * channels].reshape(
            SIDE, SIDE, channels
        )
        folded = folded.at[row_offset : row_offset + SIDE, col_offset : col_offset + SIDE].add(
            piece
        )
    return folded[1 : SIDE + 1, 1 : SIDE + 1].reshape(SIDE * SIDE, channels)


def attend(queries, key_rows, values):
    head_query = queries.reshape(queries.shape[0], HEADS, HEAD_DIM)
    head_keys = key_rows.reshape(key_rows.shape[0], HEADS, HEAD_DIM)
    head_values = values.reshape(values.shape[0], HEADS, HEAD_DIM)
    scores = jnp.einsum(
        "qhd,khd->hqk", head_query, head_keys, preferred_element_type=jnp.float32
    ) * HEAD_DIM ** (-0.5)
    maximum = jnp.max(scores, axis=2, keepdims=True)
    exponent = jnp.exp(scores - maximum)
    summed = jnp.sum(exponent, axis=2, keepdims=True)
    attended = jnp.einsum(
        "hqk,khd->qhd", lowered(exponent / summed), head_values, preferred_element_type=jnp.float32
    )
    return (
        lowered(attended.reshape(queries.shape[0], HEADS * HEAD_DIM)),
        maximum + jnp.log(summed),
    )


def attend_back(queries, key_rows, values, log_total, coarse_attended):
    head_query = queries.reshape(queries.shape[0], HEADS, HEAD_DIM)
    head_keys = key_rows.reshape(key_rows.shape[0], HEADS, HEAD_DIM)
    head_values = values.reshape(values.shape[0], HEADS, HEAD_DIM)
    head_delta = coarse_attended.reshape(queries.shape[0], HEADS, HEAD_DIM)
    scores = jnp.einsum(
        "qhd,khd->hqk", head_query, head_keys, preferred_element_type=jnp.float32
    ) * HEAD_DIM ** (-0.5)
    weights = jnp.exp(scores - log_total)
    delta_weights = jnp.einsum(
        "qhd,khd->hqk", head_delta, head_values, preferred_element_type=jnp.float32
    )
    delta_values = jnp.einsum(
        "hqk,qhd->khd", lowered(weights), head_delta, preferred_element_type=jnp.float32
    )
    delta_scores = weights * (
        delta_weights - jnp.sum(delta_weights * weights, axis=2, keepdims=True)
    )
    coarse_raw = lowered(delta_scores * HEAD_DIM ** (-0.5))
    delta_query = jnp.einsum(
        "hqk,khd->qhd", coarse_raw, head_keys, preferred_element_type=jnp.float32
    )
    delta_keys = jnp.einsum(
        "hqk,qhd->khd", coarse_raw, head_query, preferred_element_type=jnp.float32
    )
    return (
        delta_query.reshape(queries.shape[0], -1),
        delta_keys.reshape(key_rows.shape[0], -1),
        delta_values.reshape(values.shape[0], -1),
    )


def sample_pass(weights_now, latent, noise, context, timestep, region, mask_total):
    kernels, entry, middle, narrow, vectors, squares, crossing, widen = weights_now()
    table = unpack(vectors.astype(jnp.float32))
    channels = entry.shape[0]
    signal = noise_level(timestep)
    noise_value = noise.astype(jnp.float32)
    noised = jnp.sqrt(signal) * latent.astype(jnp.float32) + jnp.sqrt(1.0 - signal) * noise_value
    columns_in = neighbours(lowered(noised.T))
    hidden = product(columns_in, vectors[0:36]) + table["input_bias"]
    feature = lowered(time_features(timestep, channels))
    first_act, first_back = jax.vjp(jax.nn.silu, product(feature, entry) + table["time_in_bias"])
    first_low = lowered(first_act)
    second_act, second_back = jax.vjp(
        jax.nn.silu, product(first_low, middle) + table["middle_bias"]
    )
    second_low = lowered(second_act)
    embedding = product(second_low, narrow[0]) + table["time_out_bias"]
    act_one, back_one = jax.vjp(
        partial(norm_silu, epsilon=1e-05), hidden, table["norm_one"][0], table["norm_one"][1]
    )
    columns_one = neighbours(lowered(act_one))
    inner_act = product(columns_one, kernels[0]) + table["block_one_bias"] + embedding
    act_two, back_two = jax.vjp(
        partial(norm_silu, epsilon=1e-05), inner_act, table["norm_two"][0], table["norm_two"][1]
    )
    columns_two = neighbours(lowered(act_two))
    residual = hidden + product(columns_two, kernels[1]) + table["block_two_bias"]
    normed, back_three = jax.vjp(
        partial(group_norm, epsilon=1e-06), residual, table["norm_three"][0], table["norm_three"][1]
    )
    normed_low = lowered(normed)
    stream = product(normed_low, squares[6]) + table["project_in_bias"]
    lay_one, back_lay_one = jax.vjp(
        layer_norm, stream, table["layer_one"][0], table["layer_one"][1]
    )
    lay_one_low = lowered(lay_one)
    triple = lowered(
        product(lay_one_low, jnp.concatenate([squares[0], squares[1], squares[2]], axis=1))
    )
    attended, self_totals = attend(
        triple[:, :channels], triple[:, channels : 2 * channels], triple[:, 2 * channels :]
    )
    stream_two = stream + product(attended, squares[3]) + table["self_bias"]
    lay_two, back_lay_two = jax.vjp(
        layer_norm, stream_two, table["layer_two"][0], table["layer_two"][1]
    )
    lay_two_low = lowered(lay_two)
    cross_query = lowered(product(lay_two_low, squares[4]))
    key_value = lowered(product(context, crossing))
    cross_attended, cross_totals = attend(
        cross_query, key_value[:, :channels], key_value[:, channels:]
    )
    stream_three = stream_two + product(cross_attended, squares[5]) + table["cross_bias"]
    lay_three, back_lay_three = jax.vjp(
        layer_norm, stream_three, table["layer_three"][0], table["layer_three"][1]
    )
    lay_three_low = lowered(lay_three)
    gated_out, back_gate = jax.vjp(geglu, product(lay_three_low, widen) + table["gate_bias"])
    gated_low = lowered(gated_out)
    stream_low = lowered(stream_three + product(gated_low, narrow[1]) + table["down_bias"])
    residual_two = residual + product(stream_low, squares[7]) + table["project_out_bias"]
    act_out, back_out = jax.vjp(
        partial(norm_silu, epsilon=1e-05), residual_two, table["norm_out"][0], table["norm_out"][1]
    )
    columns_out = neighbours(lowered(act_out))
    output_kernel = (
        vectors[36:72].reshape(9, 4, channels).transpose(0, 2, 1).reshape(9 * channels, 4)
    )
    output = product(columns_out, output_kernel) + table["output_bias"]
    ratio = signal / (1.0 - signal)
    factor = jnp.minimum(ratio, 5.0) / ratio
    mismatch = output.T - noise_value
    region_value = region.astype(jnp.float32)
    loss_term = factor * jnp.sum(region_value * mismatch * mismatch) / (4.0 * mask_total)
    kernels, entry, middle, narrow, vectors, squares, crossing, widen = weights_now()
    output_kernel = (
        vectors[36:72].reshape(9, 4, channels).transpose(0, 2, 1).reshape(9 * channels, 4)
    )
    joined_qkv = jnp.concatenate([squares[0], squares[1], squares[2]], axis=1)
    coarse_output = lowered((factor * 2.0 / (4.0 * mask_total) * region_value * mismatch).T)
    output_kernel_gradient = product_left(columns_out, coarse_output)
    delta_two, out_gain, out_offset = back_out(
        fold_back(product_right(coarse_output, output_kernel), channels)
    )
    coarse_project = lowered(delta_two)
    project_out_gradient = product_left(stream_low, coarse_project)
    delta_stream = product_right(coarse_project, squares[7])
    coarse_down = lowered(delta_stream)
    down_gradient = product_left(gated_low, coarse_down)
    (delta_gated,) = back_gate(product_right(coarse_down, narrow[1]))
    coarse_gated = lowered(delta_gated)
    widen_gradient = product_left(lay_three_low, coarse_gated)
    delta_part, three_gain, three_offset = back_lay_three(product_right(coarse_gated, widen))
    delta_stream = delta_stream + delta_part
    coarse_cross = lowered(delta_stream)
    cross_out_gradient = product_left(cross_attended, coarse_cross)
    delta_query, delta_keys, delta_values = attend_back(
        cross_query,
        key_value[:, :channels],
        key_value[:, channels:],
        cross_totals,
        lowered(product_right(coarse_cross, squares[5])),
    )
    coarse_query = lowered(delta_query)
    coarse_pair = lowered(jnp.concatenate([delta_keys, delta_values], axis=1))
    cross_query_gradient = product_left(lay_two_low, coarse_query)
    crossing_gradient = product_left(context, coarse_pair)
    delta_part, two_gain, two_offset = back_lay_two(product_right(coarse_query, squares[4]))
    delta_stream = delta_stream + delta_part
    coarse_self = lowered(delta_stream)
    self_out_gradient = product_left(attended, coarse_self)
    delta_query, delta_keys, delta_values = attend_back(
        triple[:, :channels],
        triple[:, channels : 2 * channels],
        triple[:, 2 * channels :],
        self_totals,
        lowered(product_right(coarse_self, squares[3])),
    )
    coarse_triple = lowered(jnp.concatenate([delta_query, delta_keys, delta_values], axis=1))
    triple_gradient = product_left(lay_one_low, coarse_triple)
    delta_part, one_gain, one_offset = back_lay_one(product_right(coarse_triple, joined_qkv))
    coarse_stream = lowered(delta_stream + delta_part)
    project_in_gradient = product_left(normed_low, coarse_stream)
    delta_part, norm_three_gain, norm_three_offset = back_three(
        product_right(coarse_stream, squares[6])
    )
    delta_residual = delta_two + delta_part
    coarse_block_two = lowered(delta_residual)
    kernel_two_gradient = product_left(columns_two, coarse_block_two)
    delta_inner, norm_two_gain, norm_two_offset = back_two(
        fold_back(product_right(coarse_block_two, kernels[1]), channels)
    )
    coarse_inner = lowered(delta_inner)
    kernel_one_gradient = product_left(columns_one, coarse_inner)
    delta_part, norm_one_gain, norm_one_offset = back_one(
        fold_back(product_right(coarse_inner, kernels[0]), channels)
    )
    coarse_hidden = lowered(delta_residual + delta_part)
    input_kernel_gradient = product_left(columns_in, coarse_hidden)
    coarse_embedding = lowered(column_sum(coarse_inner)[None, :])
    time_out_gradient = product_left(second_low, coarse_embedding)
    (delta_second,) = second_back(product_right(coarse_embedding, narrow[0]))
    coarse_second = lowered(delta_second)
    middle_gradient = product_left(first_low, coarse_second)
    (delta_first,) = first_back(product_right(coarse_second, middle))
    coarse_first = lowered(delta_first)
    entry_gradient = product_left(feature, coarse_first)
    output_rows = (
        output_kernel_gradient.reshape(9, channels, 4).transpose(0, 2, 1).reshape(36, channels)
    )
    bias_row = jnp.pad(column_sum(coarse_output), (0, channels - 4))
    pieces = [
        input_kernel_gradient,
        output_rows,
        column_sum(coarse_hidden),
        norm_one_gain,
        norm_one_offset,
        column_sum(coarse_inner),
        column_sum(coarse_first),
        column_sum(coarse_second),
        column_sum(coarse_embedding),
        norm_two_gain,
        norm_two_offset,
        column_sum(coarse_block_two),
        norm_three_gain,
        norm_three_offset,
        column_sum(coarse_stream),
        one_gain,
        one_offset,
        column_sum(coarse_self),
        two_gain,
        two_offset,
        column_sum(coarse_cross),
        three_gain,
        three_offset,
        column_sum(coarse_gated),
        column_sum(coarse_down),
        column_sum(coarse_project),
        out_gain,
        out_offset,
        bias_row,
    ]
    vectors_gradient = jnp.concatenate([piece.reshape(-1, channels) for piece in pieces], axis=0)
    squares_gradient = jnp.stack(
        [
            triple_gradient[:, :channels],
            triple_gradient[:, channels : 2 * channels],
            triple_gradient[:, 2 * channels :],
            self_out_gradient,
            cross_query_gradient,
            cross_out_gradient,
            project_in_gradient,
            project_out_gradient,
        ]
    )
    gradients = (
        jnp.stack([kernel_one_gradient, kernel_two_gradient]),
        entry_gradient,
        middle_gradient,
        jnp.stack([time_out_gradient, down_gradient]),
        crossing_gradient,
        widen_gradient,
        vectors_gradient,
        squares_gradient,
    )
    return (loss_term, gradients)


def assemble(whole, row_parts, column_parts):
    leading = whole.shape[1:-2]
    height, breadth = whole.shape[-2:]
    depth = len(leading)
    shaped = whole.reshape((row_parts, column_parts) + leading + (height, breadth))
    order = tuple(range(2, 2 + depth)) + (0, 2 + depth, 1, 3 + depth)
    return shaped.transpose(order).reshape(leading + (row_parts * height, column_parts * breadth))


def disperse(full, row_parts, column_parts):
    leading = full.shape[:-2]
    depth = len(leading)
    height, breadth = full.shape[-2:]
    shaped = full.reshape(
        leading + (row_parts, height // row_parts, column_parts, breadth // column_parts)
    )
    order = (depth, depth + 2) + tuple(range(depth)) + (depth + 1, depth + 3)
    return shaped.transpose(order).reshape(
        (row_parts * column_parts,) + leading + (height // row_parts, breadth // column_parts)
    )


def adam(weight, first, second, gradient, rate, fix_one, fix_two):
    moment = beta_one * first + (1.0 - beta_one) * gradient
    variance = beta_two * second + (1.0 - beta_two) * gradient * gradient
    update = moment / fix_one / (jnp.sqrt(variance / fix_two) + adam_eps)
    return (weight - rate * (update + decay * weight), moment, variance)


def turned(left_basis, matrix, right_basis):
    return jnp.matmul(
        jnp.matmul(jnp.swapaxes(left_basis, 1, 2), matrix, precision=highest),
        right_basis,
        precision=highest,
    )


def orthonormal(matrix):
    gram_matrix = jnp.matmul(jnp.swapaxes(matrix, 1, 2), matrix, precision=highest)
    cholesky_factor = jnp.linalg.cholesky(gram_matrix)
    solved = jax.scipy.linalg.solve_triangular(
        cholesky_factor, jnp.swapaxes(matrix, 1, 2), lower=True
    )
    return jnp.swapaxes(solved, 1, 2)


def soap_step(gradient, state, fix_one, fix_two):
    moment = beta_one * state[0] + (1.0 - beta_one) * gradient
    rotated = turned(state[4], gradient, state[5])
    second = beta_two * state[1] + (1.0 - beta_two) * rotated * rotated
    scaled = turned(state[4], moment, state[5]) / fix_one / (jnp.sqrt(second / fix_two) + adam_eps)
    direction = jnp.matmul(
        jnp.matmul(state[4], scaled, precision=highest),
        jnp.swapaxes(state[5], 1, 2),
        precision=highest,
    )
    left_stat = beta_stat * state[2] + (1.0 - beta_stat) * jnp.matmul(
        gradient, jnp.swapaxes(gradient, 1, 2), precision=highest
    )
    right_stat = beta_stat * state[3] + (1.0 - beta_stat) * jnp.matmul(
        jnp.swapaxes(gradient, 1, 2), gradient, precision=highest
    )
    basis_left = orthonormal(jnp.matmul(left_stat, state[4], precision=highest))
    basis_right = orthonormal(jnp.matmul(right_stat, state[5], precision=highest))
    return (direction, jnp.stack([basis_left, basis_right]))


def on_device(
    latents,
    noise,
    context,
    timesteps,
    region_mask,
    owners,
    step_count,
    kernels_weight,
    kernels_first,
    kernels_second,
    entry_weight,
    entry_first,
    entry_second,
    middle_weight,
    middle_first,
    middle_second,
    narrow_weight,
    narrow_first,
    narrow_second,
    crossing_weight,
    crossing_first,
    crossing_second,
    widen_weight,
    widen_first,
    widen_second,
    vectors_weight,
    vectors_first,
    vectors_second,
    squares_weight,
    squares_state,
):
    row_parts = lax.axis_size("dp")
    column_parts = lax.axis_size("fsdp")

    def fetch():
        first_group = (
            lax.all_gather(lowered(kernels_weight)[None], ("dp", "fsdp"), axis=0, tiled=True),
            lax.all_gather(lowered(entry_weight)[None], ("dp", "fsdp"), axis=0, tiled=True),
            lax.all_gather(lowered(middle_weight)[None], ("dp", "fsdp"), axis=0, tiled=True),
            lax.all_gather(lowered(narrow_weight)[None], ("dp", "fsdp"), axis=0, tiled=True),
            lax.all_gather(lowered(vectors_weight)[None], ("dp", "fsdp"), axis=0, tiled=True),
        )
        second_group = (
            lax.all_gather(lowered(squares_weight)[None], ("dp", "fsdp"), axis=0, tiled=True),
            lax.all_gather(lowered(crossing_weight)[None], ("dp", "fsdp"), axis=0, tiled=True),
            lax.all_gather(lowered(widen_weight)[None], ("dp", "fsdp"), axis=0, tiled=True),
        )
        kernels, entry, middle, narrow, vectors = [
            assemble(piece, row_parts, column_parts) for piece in first_group
        ]
        squares, crossing, widen = [
            assemble(piece, row_parts, column_parts) for piece in second_group
        ]
        return (kernels, entry, middle, narrow, vectors, squares, crossing, widen)

    mask_total = lax.psum(jnp.sum(region_mask.astype(jnp.float32)), ("dp", "fsdp"))
    shards = (
        kernels_weight,
        entry_weight,
        middle_weight,
        narrow_weight,
        crossing_weight,
        widen_weight,
        vectors_weight,
        squares_weight,
    )
    empty = tuple(
        (
            jnp.zeros(
                piece.shape[:-2] + (piece.shape[-2] * row_parts, piece.shape[-1] * column_parts),
                jnp.float32,
            )
            for piece in shards
        )
    )

    def micro_step(carry, sample):
        sums, loss_sum = carry
        loss_term, gradients = sample_pass(
            fetch, sample[0], sample[1], sample[2], sample[3], sample[4], mask_total
        )
        return (
            (
                tuple((left_sum + right_sum for left_sum, right_sum in zip(sums, gradients))),
                loss_sum + loss_term,
            ),
            None,
        )

    samples = (latents[:, 0], noise[:, 0], context[:, 0], timesteps[:, 0], region_mask[:, 0])
    (sums, loss_sum), unused = lax.scan(micro_step, (empty, jnp.zeros((), jnp.float32)), samples)
    loss = lax.psum(loss_sum, ("dp", "fsdp"))
    steps = step_count[0].astype(jnp.float32)
    fix_one = 1.0 - jnp.power(jnp.float32(beta_one), steps)
    fix_two = 1.0 - jnp.power(jnp.float32(beta_two), steps)
    spread = [disperse(piece, row_parts, column_parts) for piece in sums]
    picker = (owners[:, None] == jnp.arange(owners.shape[0])[None, :]).astype(jnp.float32)
    reduced = (
        lax.psum_scatter(spread[0], ("dp", "fsdp"), scatter_dimension=0, tiled=True),
        lax.psum_scatter(spread[1], ("dp", "fsdp"), scatter_dimension=0, tiled=True),
        lax.psum_scatter(spread[2], ("dp", "fsdp"), scatter_dimension=0, tiled=True),
        lax.psum_scatter(spread[3], ("dp", "fsdp"), scatter_dimension=0, tiled=True),
        lax.psum_scatter(spread[4], ("dp", "fsdp"), scatter_dimension=0, tiled=True),
        lax.psum_scatter(spread[5], ("dp", "fsdp"), scatter_dimension=0, tiled=True),
        lax.psum_scatter(spread[6], ("dp", "fsdp"), scatter_dimension=0, tiled=True),
        lax.psum_scatter(spread[7], ("dp", "fsdp"), scatter_dimension=0, tiled=True),
    )
    local_square = sum((jnp.sum(piece[0] * piece[0]) for piece in reduced))
    slot_grads = jnp.einsum("sm,mab->sab", picker, reduced[7][0], precision=highest)
    arrived = lax.all_to_all(slot_grads, "fsdp", split_axis=0, concat_axis=2, tiled=True)
    owned = lax.all_gather(arrived, "dp", axis=1, tiled=True)
    grad_norm = jnp.sqrt(lax.psum(local_square, ("dp", "fsdp")))
    clip = jnp.minimum(1.0, clip_limit / grad_norm)
    squares_grad = owned * clip
    direction, squares_slots = soap_step(squares_grad, squares_state, fix_one, fix_two)
    part_rows = direction.shape[1] // row_parts
    mine = lax.dynamic_slice_in_dim(direction, lax.axis_index("dp") * part_rows, part_rows, 1)
    returned = lax.all_to_all(mine, "fsdp", split_axis=2, concat_axis=0, tiled=True)
    direction_shard = jnp.einsum("sm,sab->mab", picker, returned, precision=highest)
    rate_list = rates()
    squares_master = squares_weight - rate_list[7] * (direction_shard + decay * squares_weight)
    kernels_master, kernels_moment, kernels_variance = adam(
        kernels_weight,
        kernels_first,
        kernels_second,
        reduced[0][0] * clip,
        rate_list[0],
        fix_one,
        fix_two,
    )
    entry_master, entry_moment, entry_variance = adam(
        entry_weight,
        entry_first,
        entry_second,
        reduced[1][0] * clip,
        rate_list[1],
        fix_one,
        fix_two,
    )
    middle_master, middle_moment, middle_variance = adam(
        middle_weight,
        middle_first,
        middle_second,
        reduced[2][0] * clip,
        rate_list[2],
        fix_one,
        fix_two,
    )
    narrow_master, narrow_moment, narrow_variance = adam(
        narrow_weight,
        narrow_first,
        narrow_second,
        reduced[3][0] * clip,
        rate_list[3],
        fix_one,
        fix_two,
    )
    crossing_master, crossing_moment, crossing_variance = adam(
        crossing_weight,
        crossing_first,
        crossing_second,
        reduced[4][0] * clip,
        rate_list[4],
        fix_one,
        fix_two,
    )
    widen_master, widen_moment, widen_variance = adam(
        widen_weight,
        widen_first,
        widen_second,
        reduced[5][0] * clip,
        rate_list[5],
        fix_one,
        fix_two,
    )
    vectors_master, vectors_moment, vectors_variance = adam(
        vectors_weight,
        vectors_first,
        vectors_second,
        reduced[6][0] * clip,
        rate_list[6],
        fix_one,
        fix_two,
    )
    totals = jnp.stack([loss, grad_norm])
    return (
        totals,
        kernels_master,
        kernels_moment,
        kernels_variance,
        entry_master,
        entry_moment,
        entry_variance,
        middle_master,
        middle_moment,
        middle_variance,
        narrow_master,
        narrow_moment,
        narrow_variance,
        crossing_master,
        crossing_moment,
        crossing_variance,
        widen_master,
        widen_moment,
        widen_variance,
        vectors_master,
        vectors_moment,
        vectors_variance,
        squares_master,
        squares_slots,
        squares_grad,
    )


def solution(mesh):
    return jax.shard_map(
        on_device,
        mesh=mesh,
        in_specs=(
            P(None, ("dp", "fsdp"), None, None),
            P(None, ("dp", "fsdp"), None, None),
            P(None, ("dp", "fsdp"), None, None),
            P(None, ("dp", "fsdp")),
            P(None, ("dp", "fsdp"), None),
            P(),
            P(),
            P(None, "dp", "fsdp"),
            P(None, "dp", "fsdp"),
            P(None, "dp", "fsdp"),
            P("dp", "fsdp"),
            P("dp", "fsdp"),
            P("dp", "fsdp"),
            P("dp", "fsdp"),
            P("dp", "fsdp"),
            P("dp", "fsdp"),
            P(None, "dp", "fsdp"),
            P(None, "dp", "fsdp"),
            P(None, "dp", "fsdp"),
            P("dp", "fsdp"),
            P("dp", "fsdp"),
            P("dp", "fsdp"),
            P("dp", "fsdp"),
            P("dp", "fsdp"),
            P("dp", "fsdp"),
            P("dp", "fsdp"),
            P("dp", "fsdp"),
            P("dp", "fsdp"),
            P(None, "dp", "fsdp"),
            P(None, "fsdp", None, None),
        ),
        out_specs=(
            P(),
            P(None, "dp", "fsdp"),
            P(None, "dp", "fsdp"),
            P(None, "dp", "fsdp"),
            P("dp", "fsdp"),
            P("dp", "fsdp"),
            P("dp", "fsdp"),
            P("dp", "fsdp"),
            P("dp", "fsdp"),
            P("dp", "fsdp"),
            P(None, "dp", "fsdp"),
            P(None, "dp", "fsdp"),
            P(None, "dp", "fsdp"),
            P("dp", "fsdp"),
            P("dp", "fsdp"),
            P("dp", "fsdp"),
            P("dp", "fsdp"),
            P("dp", "fsdp"),
            P("dp", "fsdp"),
            P("dp", "fsdp"),
            P("dp", "fsdp"),
            P("dp", "fsdp"),
            P(None, "dp", "fsdp"),
            P(None, "fsdp", None, None),
            P("fsdp", None, None),
        ),
        check_vma=False,
    )
```

profile of v0, /device:TPU:0, one launch (start us, length us, event | category | flops | bytes accessed | tf_op | source)
XLA Modules:
  0.0 3991.2 jit_solution(3120225637691771262)
XLA Ops:
  10.7 42.2 %psum.21 = f32[]{:T(128)} all-reduce(f32[]{:T(128)} %convert_reduce_fusion.10), channel_id=1, replica_groups=mesh['dp'=8,'fsdp'=4] {'dp','fsdp'}, use_global_device_ids=true, to_apply=%region_1.0 | all-reduce | flops 1 | bytes 8 | tf_op jit(solution)/shard_map/psum | solution.py:536
  65.8 2367.7 %while.61 = (s32[]{:T(128)}, f32[2,2880,320]{1,2,0:T(8,128)}, f32[320,1280]{1,0:T(8,128)}, f32[1280,1280]{1,0:T(8,128)}, f32[2,1280,320]{1,2,0:T(8,128)}, /*inde...) while((s32[]{:T(128)}, f32[2,2880,320]{1,2,0:T(8,128)}, ...), condition=%wide.region_93.94_spmd.clone, body=%wide.region_2.93_spmd.clone.sunk | while | flops 31089944576 | bytes 1854688640 | solution.py:571
  75.2 67.8 %all_gather.83 = bf16[32,14,80]{2,1,0:T(8,128)(2,1)S(1)} all-gather(bf16[1,14,80]{2,1,0:T(8,128)(2,1)} %get-tuple-element.2031), channel_id=1, replica_groups=mesh['dp'=8,'fsdp'=4] {'dp','fsdp'}, dimensions={0}, use_global_device_ids=true | all-gather | bytes 73920 | tf_op jit(solution)/shard_map/while/body/eval_jaxpr/all_gather | solution.py:521
  148.6 76.1 %all_gather.82 = bf16[32,40,320]{2,1,0:T(8,128)(2,1)S(1)} all-gather(bf16[1,40,320]{2,1,0:T(8,128)(2,1)} %get-tuple-element.2035), channel_id=1, replica_groups=mesh['dp'=8,'fsdp'=4] {'dp','fsdp'}, dimensions={0}, use_global_device_ids=true | all-gather | bytes 844800 | tf_op jit(solution)/shard_map/while/body/eval_jaxpr/all_gather | solution.py:518
  230.7 86.7 %all_gather.88 = bf16[32,96,160]{1,2,0:T(8,128)(2,1)S(1)} all-gather(bf16[1,96,160]{1,2,0:T(8,128)(2,1)S(1)} %get-tuple-element.2040), channel_id=1, replica_groups=mesh['dp'=8,'fsdp'=4] {'dp','fsdp'}, dimensions={0}, use_global_device_ids=true | all-gather | bytes 1013760 | tf_op jit(solution)/shard_map/while/body/eval_jaxpr/all_gather | solution.py:525
  496.8 14.5 fusion.699
  597.5 15.4 scatter-add.211
  617.6 15.5 scatter-add.212
  642.3 14.1 scatter-add.213
  668.1 13.9 scatter-add.214
  704.7 13.7 scatter-add.216
  765.4 32.6 fusion.720
  798.0 35.8 fusion.719
  833.8 14.6 fusion.718
  898.4 15.4 scatter-add.218
  918.5 15.5 scatter-add.219
  943.3 13.9 scatter-add.220
  963.0 13.9 scatter-add.221
  1005.6 13.7 scatter-add.223
  1086.5 15.4 scatter-add.225
  1106.7 15.5 scatter-add.226
  1131.5 13.9 scatter-add.227
  1151.2 13.9 scatter-add.228
  1192.6 13.9 scatter-add.230
  1254.3 64.8 %all_gather.83 = bf16[32,14,80]{2,1,0:T(8,128)(2,1)S(1)} all-gather(bf16[1,14,80]{2,1,0:T(8,128)(2,1)} %get-tuple-element.2031), channel_id=1, replica_groups=mesh['dp'=8,'fsdp'=4] {'dp','fsdp'}, dimensions={0}, use_global_device_ids=true | all-gather | bytes 73920 | tf_op jit(solution)/shard_map/while/body/eval_jaxpr/all_gather | solution.py:521
  1324.8 77.4 %all_gather.82 = bf16[32,40,320]{2,1,0:T(8,128)(2,1)S(1)} all-gather(bf16[1,40,320]{2,1,0:T(8,128)(2,1)} %get-tuple-element.2035), channel_id=1, replica_groups=mesh['dp'=8,'fsdp'=4] {'dp','fsdp'}, dimensions={0}, use_global_device_ids=true | all-gather | bytes 844800 | tf_op jit(solution)/shard_map/while/body/eval_jaxpr/all_gather | solution.py:518
  1408.2 84.9 %all_gather.88 = bf16[32,96,160]{1,2,0:T(8,128)(2,1)S(1)} all-gather(bf16[1,96,160]{1,2,0:T(8,128)(2,1)S(1)} %get-tuple-element.2040), channel_id=1, replica_groups=mesh['dp'=8,'fsdp'=4] {'dp','fsdp'}, dimensions={0}, use_global_device_ids=true | all-gather | bytes 1013760 | tf_op jit(solution)/shard_map/while/body/eval_jaxpr/all_gather | solution.py:525
  1672.4 14.5 fusion.699
  1773.0 15.4 scatter-add.211
  1793.2 15.5 scatter-add.212
  1817.9 14.1 scatter-add.213
  1843.6 13.9 scatter-add.214
  1880.2 13.7 scatter-add.216
  1940.9 32.6 fusion.720
  1973.5 35.8 fusion.719
  2009.3 14.6 fusion.718
  2073.9 15.4 scatter-add.218
  2094.0 15.5 scatter-add.219
  2118.8 13.9 scatter-add.220
  2138.5 13.9 scatter-add.221
  2262.0 15.4 scatter-add.225
  2282.2 15.5 scatter-add.226
  2307.0 13.9 scatter-add.227
  2326.7 13.9 scatter-add.228
  2368.2 13.9 scatter-add.230
  2518.4 43.7 %all-reduce.20.cloned.1.call-done = f32[32,14,80]{2,0,1:T(8,128)} async-done(((f32[32,14,80]{2,0,1:T(8,128)}), f32[32,14,80]{2,0,1:T(8,128)}) %all-reduce.20.cloned.1.call-update) | async-done | bytes 143376
  2563.6 103.4 %reduce-scatter.24.cloned.1.call-done = f32[1,40,320]{2,1,0:T(8,128)} async-done(((f32[32,40,320]{2,1,0:T(8,128)}), f32[1,40,320]{2,1,0:T(8,128)}) %reduce-scatter.24.cloned.1.call-update) | async-done | bytes 51216
  2668.4 141.1 %reduce-scatter.20.cloned.1.call-done = f32[1,96,160]{1,2,0:T(8,128)} async-done(((f32[32,96,160]{1,2,0:T(8,128)}), f32[1,96,160]{1,2,0:T(8,128)}) %reduce-scatter.20.cloned.1.call-update) | async-done | bytes 61456 | tf_op jit(solution)/shard_map/reduce_scatter | solution.py:583
  2811.1 153.9 %reduce-scatter.22.cloned.1.call-done = f32[1,8,40,80]{3,1,2,0:T(8,128)} async-done(((f32[32,8,40,80]{3,1,2,0:T(8,128)}), f32[1,8,40,80]{3,1,2,0:T(8,128)}) %reduce-scatter.22.cloned.1.call-update) | async-done | bytes 102416 | tf_op jit(solution)/shard_map/reduce_scatter | solution.py:586
  2971.8 139.2 %reduce-scatter.26.cloned.1.call-done = f32[1,40,640]{2,1,0:T(8,128)} async-done(((f32[32,40,640]{2,1,0:T(8,128)}), f32[1,40,640]{2,1,0:T(8,128)}) %reduce-scatter.26.cloned.1.call-update) | async-done | bytes 102416
  3112.5 154.2 %reduce-scatter.18.cloned.1.call-done = f32[1,2,160,80]{3,2,1,0:T(8,128)} async-done(((f32[32,2,160,80]{3,2,1,0:T(8,128)}), f32[1,2,160,80]{3,2,1,0:T(8,128)}) %reduce-scatter.18.cloned.1.call-update) | async-done | bytes 102416 | tf_op jit(solution)/shard_map/reduce_scatter | solution.py:582
  3279.5 114.3 %reduce-scatter.16.cloned.1.call-done = f32[1,160,320]{2,1,0:T(8,128)} async-done(((f32[32,160,320]{2,1,0:T(8,128)}), f32[1,160,320]{2,1,0:T(8,128)}) %reduce-scatter.16.cloned.1.call-update) | async-done | bytes 204816 | tf_op jit(solution)/shard_map/reduce_scatter | solution.py:581
  3395.4 125.9 %reduce-scatter.14.cloned.1.call-done = f32[1,2,360,80]{2,3,1,0:T(8,128)} async-done(((f32[32,2,360,80]{2,3,1,0:T(8,128)}), f32[1,2,360,80]{2,3,1,0:T(8,128)}) %reduce-scatter.14.cloned.1.call-update) | async-done | bytes 230416 | tf_op jit(solution)/shard_map/reduce_scatter | solution.py:579
  3528.0 40.5 %all-reduce.17 = (f32[]{:T(128)}, f32[1]{0:T(128)}) all-reduce(f32[]{:T(128)S(6)} %add.1267, f32[1]{0:T(128)} %bitcast.12), channel_id=1, replica_groups=mesh['dp'=8,'fsdp'=4] {'dp','fsdp'}, use_global_device_ids=true, to_apply=%region_111.112 | all-reduce | flops 2 | bytes 16 | tf_op jit(solution)/shard_map/psum | solution.py:592
  3604.8 23.7 custom-call.40
  3646.0 23.5 custom-call.34
  3669.6 19.7 custom-call.35
  3689.3 19.7 custom-call.41
  3711.6 23.6 custom-call.42
  3737.9 23.5 custom-call.36
  3761.4 19.7 custom-call.43
  3794.2 19.9 custom-call.37
  3839.9 60.4 %custom-call.39 = f32[2,3,128,128]{2,3,1,0:T(8,128)} custom-call(f32[2,3,128,128]{3,2,1,0:T(8,128)} %pad_maximum_fusion.8), custom_call_target="InvertDiagBlocksLowerTriangular" | custom-call | tf_op jit(solution)/shard_map/jit(_solve_triangular)/vmap()/triangular_solve | solution.py:453
  3900.4 59.8 %custom-call.45 = f32[2,3,128,128]{2,3,1,0:T(8,128)} custom-call(f32[2,3,128,128]{3,2,1,0:T(8,128)S(1)} %pad_maximum_fusion.9), custom_call_target="InvertDiagBlocksLowerTriangular" | custom-call | tf_op jit(solution)/shard_map/jit(_solve_triangular)/vmap()/triangular_solve | solution.py:453
  (2195 shorter events, 1526.4 us)
Async XLA Ops:
  8.0 56.4 %copy-start.209 = (bf16[2,1,77,768]{3,0,2,1:T(2,128)(2,1)S(1)}, bf16[2,1,77,768]{3,0,2,1:T(2,128)(2,1)}, u32[]{:S(2)}) copy-start(bf16[2,1,77,768]{3,0,2,1:T(2,128)(2,1)} %param.91) | copy-start | bytes 709636
  66.0 164.7 %copy-start.146 = (bf16[1,96,160]{1,2,0:T(8,128)(2,1)}, bf16[1,96,160]{1,2,0:T(8,128)(2,1)S(1)}, u32[]{:S(2)}) copy-start(bf16[1,96,160]{1,2,0:T(8,128)(2,1)S(1)} %get-tuple-element.2040) | copy-start | bytes 92164 | tf_op jit(solution)/shard_map/while
  66.0 287.2 %all-gather.14.cloned.1.call-start = ((), (), s32[]{:S(2)}) async-start(), calls=%async_computation.21 | async-start | bytes 1689600 | tf_op jit(solution)/shard_map/while/body/eval_jaxpr/all_gather | solution.py:526
  66.7 290.0 %all-gather.12.cloned.1.call-start = ((), (), s32[]{:S(2)}) async-start(), calls=%async_computation.20 | async-start | bytes 2703360 | tf_op jit(solution)/shard_map/while/body/eval_jaxpr/all_gather | solution.py:524
  67.5 297.2 %all-gather.8.cloned.1.call-start = ((), (), s32[]{:S(2)}) async-start(), calls=%async_computation.18 | async-start | bytes 2703360 | tf_op jit(solution)/shard_map/while/body/eval_jaxpr/all_gather | solution.py:520
  68.2 323.4 %all-gather.6.cloned.1.call-start = ((), (), s32[]{:S(2)}) async-start(), calls=%async_computation.17 | async-start | bytes 4055040 | tf_op jit(solution)/shard_map/while/body/eval_jaxpr/all_gather | solution.py:519
  68.8 340.7 %all-gather.10.cloned.1.call-start = ((), (), s32[]{:S(2)}) async-start(), calls=%async_computation.19 | async-start | bytes 4055040 | tf_op jit(solution)/shard_map/while/body/eval_jaxpr/all_gather | solution.py:517
  143.2 84.2 %copy-start.113 = (f32[112,320]{1,0:T(8,128)}, f32[112,320]{1,0:T(8,128)S(1)}, u32[]{:S(2)}) copy-start(f32[112,320]{1,0:T(8,128)S(1)} %convert_element_type.955) | copy-start | bytes 430084 | tf_op jit(solution)/shard_map/while
  227.5 120.5 %copy-start.158 = (f32[320]{0:T(512)}, f32[320]{0:T(512)S(1)}, u32[]{:S(2)}) copy-start(f32[320]{0:T(512)S(1)} %get-tuple-element.1766) | copy-start | bytes 3844 | tf_op jit(solution)/shard_map/while
  228.0 232.3 %copy-start = (f32[1024,320]{0,1:T(8,128)}, f32[1024,320]{0,1:T(8,128)S(1)}, u32[]{:S(2)}) copy-start(f32[1024,320]{0,1:T(8,128)S(1)} %get-tuple-element.1764) | copy-start | bytes 3932164 | tf_op jit(solution)/shard_map/while
  228.4 119.6 %copy-start.135 = (f32[320]{0:T(512)}, f32[320]{0:T(512)S(1)}, u32[]{:S(2)}) copy-start(f32[320]{0:T(512)S(1)} %sub.962) | copy-start | bytes 3844 | tf_op jit(solution)/shard_map/while
  229.7 118.4 %copy-start.148 = (f32[320]{0:T(512)}, f32[320]{0:T(512)S(1)}, u32[]{:S(2)}) copy-start(f32[320]{0:T(512)S(1)} %mul.3333) | copy-start | bytes 3844 | tf_op jit(solution)/shard_map/while
  345.7 112.1 %copy-start.150 = (f32[320]{0:T(512)}, f32[320]{0:T(512)S(1)}, u32[]{:S(2)}) copy-start(f32[320]{0:T(512)S(1)} %get-tuple-element.1778) | copy-start | bytes 3844 | tf_op jit(solution)/shard_map/while
  375.6 32.9 copy-start.34
  428.4 29.5 copy-start.2
  428.9 29.0 copy-start.137
  430.1 27.8 copy-start.152
  464.7 70.6 %copy-start.9 = (f32[1024,320]{0,1:T(8,128)}, f32[1024,320]{0,1:T(8,128)S(1)}, u32[]{:S(2)}) copy-start(f32[1024,320]{0,1:T(8,128)S(1)} %get-tuple-element.1791) | copy-start | bytes 3932164 | tf_op jit(solution)/shard_map/while
  467.3 44.1 %copy-start.17 = (f32[1024,320]{0,1:T(8,128)}, f32[1024,320]{0,1:T(8,128)S(1)}, u32[]{:S(2)}) copy-start(f32[1024,320]{0,1:T(8,128)S(1)} %get-tuple-element.1799) | copy-start | bytes 3932164 | tf_op jit(solution)/shard_map/while
  469.5 27.4 copy-start.102
  517.2 16.7 copy-start.14
  517.2 227.5 %copy-start.142 = (f32[1024]{0:T(1024)}, f32[1024]{0:T(1024)S(1)}, u32[]{:S(2)}) copy-start(f32[1024]{0:T(1024)S(1)} %broadcast_multiply_fusion.23) | copy-start | bytes 12292 | tf_op jit(solution)/shard_map/while
  765.3 32.7 copy-start.55
  833.8 14.6 copy-start.197
  833.8 14.6 copy-start.221
  1039.5 14.8 copy-start.276
  1245.1 163.0 %copy-start.146 = (bf16[1,96,160]{1,2,0:T(8,128)(2,1)}, bf16[1,96,160]{1,2,0:T(8,128)(2,1)S(1)}, u32[]{:S(2)}) copy-start(bf16[1,96,160]{1,2,0:T(8,128)(2,1)S(1)} %get-tuple-element.2040) | copy-start | bytes 92164 | tf_op jit(solution)/shard_map/while
  1245.1 283.7 %all-gather.14.cloned.1.call-start = ((), (), s32[]{:S(2)}) async-start(), calls=%async_computation.21 | async-start | bytes 1689600 | tf_op jit(solution)/shard_map/while/body/eval_jaxpr/all_gather | solution.py:526
  1245.7 286.6 %all-gather.12.cloned.1.call-start = ((), (), s32[]{:S(2)}) async-start(), calls=%async_computation.20 | async-start | bytes 2703360 | tf_op jit(solution)/shard_map/while/body/eval_jaxpr/all_gather | solution.py:524
  1246.5 293.9 %all-gather.8.cloned.1.call-start = ((), (), s32[]{:S(2)}) async-start(), calls=%async_computation.18 | async-start | bytes 2703360 | tf_op jit(solution)/shard_map/while/body/eval_jaxpr/all_gather | solution.py:520
  1247.2 319.9 %all-gather.6.cloned.1.call-start = ((), (), s32[]{:S(2)}) async-start(), calls=%async_computation.17 | async-start | bytes 4055040 | tf_op jit(solution)/shard_map/while/body/eval_jaxpr/all_gather | solution.py:519
  1247.9 337.1 %all-gather.10.cloned.1.call-start = ((), (), s32[]{:S(2)}) async-start(), calls=%async_computation.19 | async-start | bytes 4055040 | tf_op jit(solution)/shard_map/while/body/eval_jaxpr/all_gather | solution.py:517
  1319.4 85.5 %copy-start.113 = (f32[112,320]{1,0:T(8,128)}, f32[112,320]{1,0:T(8,128)S(1)}, u32[]{:S(2)}) copy-start(f32[112,320]{1,0:T(8,128)S(1)} %convert_element_type.955) | copy-start | bytes 430084 | tf_op jit(solution)/shard_map/while
  1405.0 118.7 %copy-start.158 = (f32[320]{0:T(512)}, f32[320]{0:T(512)S(1)}, u32[]{:S(2)}) copy-start(f32[320]{0:T(512)S(1)} %get-tuple-element.1766) | copy-start | bytes 3844 | tf_op jit(solution)/shard_map/while
  1405.5 230.4 %copy-start = (f32[1024,320]{0,1:T(8,128)}, f32[1024,320]{0,1:T(8,128)S(1)}, u32[]{:S(2)}) copy-start(f32[1024,320]{0,1:T(8,128)S(1)} %get-tuple-element.1764) | copy-start | bytes 3932164 | tf_op jit(solution)/shard_map/while
  1405.9 117.8 %copy-start.135 = (f32[320]{0:T(512)}, f32[320]{0:T(512)S(1)}, u32[]{:S(2)}) copy-start(f32[320]{0:T(512)S(1)} %sub.962) | copy-start | bytes 3844 | tf_op jit(solution)/shard_map/while
  1407.2 116.5 %copy-start.148 = (f32[320]{0:T(512)}, f32[320]{0:T(512)S(1)}, u32[]{:S(2)}) copy-start(f32[320]{0:T(512)S(1)} %mul.3333) | copy-start | bytes 3844 | tf_op jit(solution)/shard_map/while
  1521.4 112.0 %copy-start.150 = (f32[320]{0:T(512)}, f32[320]{0:T(512)S(1)}, u32[]{:S(2)}) copy-start(f32[320]{0:T(512)S(1)} %get-tuple-element.1778) | copy-start | bytes 3844 | tf_op jit(solution)/shard_map/while
  1551.1 32.9 copy-start.34
  1604.0 29.5 copy-start.2
  1604.4 29.0 copy-start.137
  1605.6 27.8 copy-start.152
  1640.2 70.6 %copy-start.9 = (f32[1024,320]{0,1:T(8,128)}, f32[1024,320]{0,1:T(8,128)S(1)}, u32[]{:S(2)}) copy-start(f32[1024,320]{0,1:T(8,128)S(1)} %get-tuple-element.1791) | copy-start | bytes 3932164 | tf_op jit(solution)/shard_map/while
  1642.8 44.1 %copy-start.17 = (f32[1024,320]{0,1:T(8,128)}, f32[1024,320]{0,1:T(8,128)S(1)}, u32[]{:S(2)}) copy-start(f32[1024,320]{0,1:T(8,128)S(1)} %get-tuple-element.1799) | copy-start | bytes 3932164 | tf_op jit(solution)/shard_map/while
  1645.0 27.4 copy-start.102
  1692.7 16.7 copy-start.14
  1692.7 227.5 %copy-start.142 = (f32[1024]{0:T(1024)}, f32[1024]{0:T(1024)S(1)}, u32[]{:S(2)}) copy-start(f32[1024]{0:T(1024)S(1)} %broadcast_multiply_fusion.23) | copy-start | bytes 12292 | tf_op jit(solution)/shard_map/while
  1940.9 32.7 copy-start.55
  2009.3 14.6 copy-start.197
  2215.0 14.8 copy-start.276
  2433.5 128.6 %all-reduce.20.cloned.1.call-start = ((), (), s32[]{:S(2)}) async-start(), calls=%async_computation.14 | async-start | bytes 458752
  2435.5 231.5 %reduce-scatter.24.cloned.1.call-start = ((), (), s32[]{:S(2)}) async-start(), calls=%async_computation.15 | async-start | bytes 2027520
  2439.6 370.0 %reduce-scatter.20.cloned.1.call-start = ((), (), s32[]{:S(2)}) async-start(), calls=%async_computation.12 | async-start | bytes 2703360 | tf_op jit(solution)/shard_map/reduce_scatter | solution.py:583
  2447.7 517.2 %reduce-scatter.22.cloned.1.call-start = ((), (), s32[]{:S(2)}) async-start(), calls=%async_computation.13 | async-start | bytes 5406720 | tf_op jit(solution)/shard_map/reduce_scatter | solution.py:586
  2462.1 648.9 %reduce-scatter.26.cloned.1.call-start = ((), (), s32[]{:S(2)}) async-start(), calls=%async_computation.16 | async-start | bytes 3379200
  2467.5 799.3 %reduce-scatter.18.cloned.1.call-start = ((), (), s32[]{:S(2)}) async-start(), calls=%async_computation.11 | async-start | bytes 5406720 | tf_op jit(solution)/shard_map/reduce_scatter | solution.py:582
  2480.0 913.8 %reduce-scatter.16.cloned.1.call-start = ((), (), s32[]{:S(2)}) async-start(), calls=%async_computation.10 | async-start | bytes 8110080 | tf_op jit(solution)/shard_map/reduce_scatter | solution.py:581
  2497.4 1023.8 %reduce-scatter.14.cloned.1.call-start = ((), (), s32[]{:S(2)}) async-start(), calls=%async_computation.9 | async-start | bytes 8110080 | tf_op jit(solution)/shard_map/reduce_scatter | solution.py:579
  2516.9 448.0 %copy-start.290 = (s32[8]{0:T(128)S(1)}, s32[8]{0:T(128)}, u32[]{:S(2)}) copy-start(s32[8]{0:T(128)} %param.94) | copy-start | bytes 100
  2966.9 301.4 %all-to-all-start = ((f32[8,40,80]{2,1,0:T(8,128)}), f32[8,40,80]{2,1,0:T(8,128)S(1)}, u32[]{:S(2)}, u32[]{:S(2)}) async-start(f32[8,40,80]{2,1,0:T(8,128)} %copy.689), calls=%async_computation.5 | async-start | bytes 327680 | tf_op jit(solution)/shard_map/all_to_all | solution.py:590
  3602.4 26.0 copy-start.130
  3641.8 338.6 %all-to-all-start.1 = ((f32[4,1,6400]{2,1,0:T(1,128)}), f32[4,1,6400]{2,1,0:T(1,128)S(1)}, u32[]{:S(2)}, u32[]{:S(2)}) async-start(f32[4,1,6400]{2,1,0:T(1,128)} %reshape.2931), calls=%async_computation.6 | async-start | bytes 204800 | tf_op jit(solution)/shard_map/all_to_all | solution.py:598
  3646.0 65.6 %copy-start.134 = (f32[2,320,320]{2,1,0:T(8,128)}, f32[2,320,320]{2,1,0:T(8,128)S(1)}, u32[]{:S(2)}) copy-start(f32[2,320,320]{2,1,0:T(8,128)S(1)} %fusion.175) | copy-start | bytes 2457604
  3835.0 125.3 %copy-start.128 = (f32[2,320,320]{1,2,0:T(8,128)S(1)}, f32[2,320,320]{1,2,0:T(8,128)}, u32[]{:S(2)}) copy-start(f32[2,320,320]{1,2,0:T(8,128)} %copy.708) | copy-start | bytes 2457604
  (516 other events, 1913.7 us)
Sparse Core Ops, SparseCore 0:
  70.2 55.3 all-gather.13
  129.0 58.2 all-gather.11
  190.6 58.4 all-gather.7
  252.3 62.2 all-gather.5
  317.9 60.5 all-gather.9
  1249.0 52.1 all-gather.13
  1304.6 57.7 all-gather.11
  1365.9 57.7 all-gather.7
  1427.1 61.8 all-gather.5
  1492.3 60.4 all-gather.9
Sparse Core Ops, SparseCore 1:
  2440.1 121.9 all-reduce.19
  2567.2 99.7 reduce-scatter.23
  2669.1 140.4 reduce-scatter.19
  2811.9 153.0 reduce-scatter.21
  2967.3 143.7 reduce-scatter.25
  3113.3 153.4 reduce-scatter.17
  3272.3 121.5 reduce-scatter.15
  3399.3 121.9 reduce-scatter.13
where the time goes:
time: 4010 us; the launch traced here: 3990 us
  local copies, waits for them, and re-layouts  1260 us (31%)
  waiting for transfers between devices  982 us (24%)
  other arithmetic  632 us (16%)
  blocking collectives  550 us (14%)
  matrix products  511 us (13%)
    scatter-add x42, local copies, waits for them, and re-layouts, fold_back(): folded.at[row_offset:row_offset + SIDE, col_offset:col_offset + SIDE]  527 us
    unnamed x11, waiting for transfers between devices  286 us
    slice x60, local copies, waits for them, and re-layouts, fold_back(): columns[:, tap_index * channels:(tap_index + 1) * channels]  203 us
    another operation x21, other arithmetic, orthonormal(): cholesky_factor = jnp.linalg.cholesky(gram_matrix)  197 us
    all_gather x2, blocking collectives, fetch(): lax.all_gather(lowered(crossing_weight)[None], ('dp', 'fsdp'), axis=0, ti...  172 us
    reduce_scatter x1, waiting for transfers between devices, on_device(): lax.psum_scatter(spread[3], ('dp', 'fsdp'), scatter_dimension=0, tiled=True)  154 us
    reduce_scatter x1, waiting for transfers between devices, on_device(): lax.psum_scatter(spread[7], ('dp', 'fsdp'), scatter_dimension=0, tiled=True)  154 us
    all_gather x2, blocking collectives, fetch(): lax.all_gather(lowered(entry_weight)[None], ('dp', 'fsdp'), axis=0, tiled...  154 us
  transfers between devices with their start and end apart: 20, of which 8 were waited for; matrix products, arithmetic and copies ran while one was open for 16% of the time, Pallas kernels for 0%

commit v1 on v0

v1 whole, which is shorter than its diff:
```python
from functools import partial
import math

import jax
import jax.numpy as jnp
from jax import lax
from jax.experimental import pallas as pl
from jax.experimental.pallas import tpu as pltpu
from jax.sharding import PartitionSpec as P

C = 320
HEADS = 8
GROUPS = 32
CTX_DIM = 768
SIDE = 32
HEAD_DIM = 40


highest = lax.Precision.HIGHEST
beta_one = 0.9
beta_two = 0.999
beta_stat = 0.95
adam_eps = 1e-08
decay = 0.01
clip_limit = 0.002


def lowered(values):
    return values.astype(jnp.bfloat16)


def product(left_matrix, right_matrix):
    return jnp.dot(left_matrix, right_matrix, preferred_element_type=jnp.float32)


def product_left(left_matrix, right_matrix):
    return lax.dot_general(
        left_matrix, right_matrix, (((0,), (0,)), ((), ())), preferred_element_type=jnp.float32
    )


def product_right(left_matrix, right_matrix):
    return lax.dot_general(
        left_matrix, right_matrix, (((1,), (1,)), ((), ())), preferred_element_type=jnp.float32
    )


def column_sum(values):
    return jnp.sum(values.astype(jnp.float32), axis=0)


def rates():
    return (
        3.0 / math.sqrt(9 * C),
        3.0 / math.sqrt(C),
        3.0 / math.sqrt(4 * C),
        3.0 / math.sqrt(4 * C),
        3.0 / math.sqrt(CTX_DIM),
        3.0 / math.sqrt(C),
        0.3,
        3.0 / math.sqrt(C),
    )


def noise_level(timestep):
    levels = jnp.arange(1000, dtype=jnp.float32)
    roots = 0.00085**0.5 + (0.012**0.5 - 0.00085**0.5) * levels / 999.0
    signals = jnp.exp(jnp.cumsum(jnp.log1p(-roots * roots)))
    return jnp.sum(jnp.where(jnp.arange(1000) == timestep, signals, 0.0))


def time_features(timestep, channels):
    halfway = channels // 2
    freqs = jnp.exp(-math.log(10000.0) * jnp.arange(halfway, dtype=jnp.float32) / halfway)
    angles = timestep.astype(jnp.float32) * freqs
    return jnp.concatenate([jnp.cos(angles), jnp.sin(angles)])[None, :]


def unpack(vector_table):
    return dict(
        input_bias=vector_table[72],
        norm_one=vector_table[73:75],
        block_one_bias=vector_table[75],
        time_in_bias=vector_table[76:80].reshape(-1),
        middle_bias=vector_table[80:84].reshape(-1),
        time_out_bias=vector_table[84],
        norm_two=vector_table[85:87],
        block_two_bias=vector_table[87],
        norm_three=vector_table[88:90],
        project_in_bias=vector_table[90],
        layer_one=vector_table[91:93],
        self_bias=vector_table[93],
        layer_two=vector_table[94:96],
        cross_bias=vector_table[96],
        layer_three=vector_table[97:99],
        gate_bias=vector_table[99:107].reshape(-1),
        down_bias=vector_table[107],
        project_out_bias=vector_table[108],
        norm_out=vector_table[109:111],
        output_bias=vector_table[111, 0:4],
    )


GROUP = 10
WIDE = 384
LANES = 128
QUERY_BLOCK = 256
LOG2E = 1.4426950408889634


def wide_columns(matrix):
    lead = matrix.shape[0]
    parts = []
    for start, stop in ((0, 120), (120, 240), (240, 320)):
        parts.append(
            jnp.pad(matrix[:, start:stop], ((0, 0), (0, LANES - (stop - start))))
        )
    return jnp.concatenate(parts, axis=1).reshape(lead, WIDE)


def wide_rows(matrix):
    parts = []
    for start, stop in ((0, 120), (120, 240), (240, 320)):
        parts.append(jnp.pad(matrix[start:stop], ((0, LANES - (stop - start)), (0, 0))))
    return jnp.concatenate(parts, axis=0)


def slim_columns(matrix):
    return jnp.concatenate(
        [matrix[:, 0:120], matrix[:, 128:248], matrix[:, 256:336]], axis=1
    )


def slim_rows(matrix):
    return jnp.concatenate([matrix[0:120], matrix[128:248], matrix[256:336]], axis=0)


def dot_nt(left_matrix, right_matrix):
    return lax.dot_general(
        left_matrix, right_matrix, (((1,), (1,)), ((), ())), preferred_element_type=jnp.float32
    )


def dot_nn(left_matrix, right_matrix):
    return lax.dot_general(
        left_matrix, right_matrix, (((1,), (0,)), ((), ())), preferred_element_type=jnp.float32
    )


def attend_kernel(valid, q_ref, k_ref, vt_ref, out_ref, total_ref):
    tile = pl.program_id(1)
    member = pl.program_id(3)
    scaling = HEAD_DIM ** (-0.5) * LOG2E

    @pl.when(tile * 3 + member < HEADS)
    def _():
        low_lane = member * HEAD_DIM
        lane = lax.broadcasted_iota(jnp.int32, (QUERY_BLOCK, LANES), 1)
        chosen = (lane >= low_lane) & (lane < low_lane + HEAD_DIM)
        query = jnp.where(chosen, q_ref[...], jnp.zeros((), jnp.bfloat16))
        scores = dot_nt(k_ref[...], query)
        if valid < scores.shape[0]:
            row = lax.broadcasted_iota(jnp.int32, scores.shape, 0)
            scores = jnp.where(row < valid, scores, -1e30)
        maximum = jnp.max(scores, axis=0, keepdims=True) * scaling
        exponent = jnp.exp2(scores * scaling - maximum)
        summed = jnp.sum(exponent, axis=0, keepdims=True)
        weights = (exponent * (1.0 / summed)).astype(jnp.bfloat16)
        attended = dot_nn(vt_ref[...], weights)
        row = lax.broadcasted_iota(jnp.int32, attended.shape, 0)
        inside = (row >= low_lane) & (row < low_lane + HEAD_DIM)
        earlier = jnp.where(member == 0, 0.0, out_ref[...].astype(jnp.float32))
        out_ref[...] = jnp.where(inside, attended, earlier).astype(jnp.bfloat16)
        total_ref[pl.ds(member, 1), :] = maximum + jnp.log2(summed)


def attend(queries, key_rows, values_turned, valid):
    samples, pixels, wide = queries.shape
    keys = key_rows.shape[1]
    blocks = pixels // QUERY_BLOCK
    return pl.pallas_call(
        partial(attend_kernel, valid),
        grid=(samples, wide // LANES, blocks, 3),
        in_specs=[
            pl.BlockSpec((None, QUERY_BLOCK, LANES), lambda s, t, b, j: (s, b, t)),
            pl.BlockSpec((None, keys, LANES), lambda s, t, b, j: (s, 0, t)),
            pl.BlockSpec((None, LANES, keys), lambda s, t, b, j: (s, t, 0)),
        ],
        out_specs=[
            pl.BlockSpec((None, LANES, QUERY_BLOCK), lambda s, t, b, j: (s, t, b)),
            pl.BlockSpec((None, None, 8, QUERY_BLOCK), lambda s, t, b, j: (s, t, 0, b)),
        ],
        out_shape=[
            jax.ShapeDtypeStruct((samples, wide, pixels), jnp.bfloat16),
            jax.ShapeDtypeStruct((samples, wide // LANES, 8, pixels), jnp.float32),
        ],
        compiler_params=pltpu.CompilerParams(vmem_limit_bytes=24 * 1024 * 1024),
        cost_estimate=pl.CostEstimate(
            flops=samples * HEADS * pixels * keys * 512,
            bytes_accessed=samples * pixels * wide * 8,
            transcendentals=samples * HEADS * pixels * keys,
        ),
        name="attend",
    )(queries, key_rows, values_turned)


def attend_back_kernel(
    valid,
    q_ref,
    k_ref,
    kt_ref,
    v_ref,
    delta_ref,
    total_ref,
    dq_ref,
    dk_ref,
    dv_ref,
    dk_sum,
    dv_sum,
):
    tile = pl.program_id(1)
    block = pl.program_id(2)
    member = pl.program_id(3)
    scaling = HEAD_DIM ** (-0.5) * LOG2E

    @pl.when((block == 0) & (member == 0))
    def _():
        dk_sum[...] = jnp.zeros_like(dk_sum)
        dv_sum[...] = jnp.zeros_like(dv_sum)

    @pl.when(tile * 3 + member < HEADS)
    def _():
        low_lane = member * HEAD_DIM
        lane = lax.broadcasted_iota(jnp.int32, (QUERY_BLOCK, LANES), 1)
        chosen = (lane >= low_lane) & (lane < low_lane + HEAD_DIM)
        query = jnp.where(chosen, q_ref[...], jnp.zeros((), jnp.bfloat16))
        row = lax.broadcasted_iota(jnp.int32, (LANES, QUERY_BLOCK), 0)
        inside = (row >= low_lane) & (row < low_lane + HEAD_DIM)
        delta = jnp.where(inside, delta_ref[...], jnp.zeros((), jnp.bfloat16))
        scores = dot_nt(k_ref[...], query)
        weights = jnp.exp2(scores * scaling - total_ref[pl.ds(member, 1), :])
        if valid < scores.shape[0]:
            key_row = lax.broadcasted_iota(jnp.int32, scores.shape, 0)
            weights = jnp.where(key_row < valid, weights, 0.0)
        delta_weights = dot_nn(v_ref[...], delta)
        dv_sum[...] += dot_nt(weights.astype(jnp.bfloat16), delta)
        middle = jnp.sum(delta_weights * weights, axis=0, keepdims=True)
        coarse = (weights * (delta_weights - middle) * HEAD_DIM ** (-0.5)).astype(jnp.bfloat16)
        dk_sum[...] += dot_nn(coarse, query)
        delta_query = dot_nn(kt_ref[...], coarse)
        earlier = jnp.where(member == 0, 0.0, dq_ref[...].astype(jnp.float32))
        dq_ref[...] = jnp.where(inside, delta_query, earlier).astype(jnp.bfloat16)

    @pl.when((block == pl.num_programs(2) - 1) & (member == 2))
    def _():
        dk_ref[...] = dk_sum[...].astype(jnp.bfloat16)
        dv_ref[...] = dv_sum[...].astype(jnp.bfloat16)


def attend_back(queries, key_rows, keys_turned, values, delta_turned, totals, valid):
    samples, pixels, wide = queries.shape
    keys = key_rows.shape[1]
    blocks = pixels // QUERY_BLOCK
    key_spec = pl.BlockSpec((None, keys, LANES), lambda s, t, b, j: (s, 0, t))
    turned_spec = pl.BlockSpec((None, LANES, QUERY_BLOCK), lambda s, t, b, j: (s, t, b))
    return pl.pallas_call(
        partial(attend_back_kernel, valid),
        grid=(samples, wide // LANES, blocks, 3),
        in_specs=[
            pl.BlockSpec((None, QUERY_BLOCK, LANES), lambda s, t, b, j: (s, b, t)),
            key_spec,
            pl.BlockSpec((None, LANES, keys), lambda s, t, b, j: (s, t, 0)),
            key_spec,
            turned_spec,
            pl.BlockSpec((None, None, 8, QUERY_BLOCK), lambda s, t, b, j: (s, t, 0, b)),
        ],
        out_specs=[turned_spec, key_spec, key_spec],
        out_shape=[
            jax.ShapeDtypeStruct((samples, wide, pixels), jnp.bfloat16),
            jax.ShapeDtypeStruct((samples, keys, wide), jnp.bfloat16),
            jax.ShapeDtypeStruct((samples, keys, wide), jnp.bfloat16),
        ],
        scratch_shapes=[pltpu.VMEM((keys, LANES), jnp.float32)] * 2,
        compiler_params=pltpu.CompilerParams(vmem_limit_bytes=24 * 1024 * 1024),
        cost_estimate=pl.CostEstimate(
            flops=samples * HEADS * pixels * keys * 1280,
            bytes_accessed=samples * pixels * wide * 16,
            transcendentals=samples * HEADS * pixels * keys,
        ),
        name="attend_back",
    )(queries, key_rows, keys_turned, values, delta_turned, totals)


def group_spread(sums, count):
    channels = sums.shape[-1]
    index = jnp.arange(channels) // GROUP
    mixer = (index[:, None] == index[None, :]).astype(jnp.float32)
    return jnp.matmul(sums, mixer, precision=highest) / count


def group_stats(values, epsilon):
    count = values.shape[1] * GROUP
    average = group_spread(jnp.sum(values, axis=1), count)[:, None, :]
    spread = group_spread(jnp.sum(jnp.square(values - average), axis=1), count)[:, None, :]
    return average, lax.rsqrt(spread + epsilon)


def group_apply(values, stats, gains):
    return (values - stats[0]) * stats[1] * gains[0] + gains[1]


def group_back(values, stats, gains, delta):
    count = values.shape[1] * GROUP
    normal = (values - stats[0]) * stats[1]
    offset_sum = jnp.sum(delta, axis=1)
    gain_sum = jnp.sum(delta * normal, axis=1)
    first = group_spread(offset_sum * gains[0], count)[:, None, :]
    second = group_spread(gain_sum * gains[0], count)[:, None, :]
    result = stats[1] * (delta * gains[0] - first - normal * second)
    return result, jnp.sum(gain_sum, axis=0), jnp.sum(offset_sum, axis=0)


def silu_slope(values, delta):
    gate = jax.nn.sigmoid(values)
    return delta * gate * (1.0 + values * (1.0 - gate))


def layer_norm(values, gains):
    average = jnp.mean(values, axis=-1, keepdims=True)
    spread = jnp.mean(jnp.square(values - average), axis=-1, keepdims=True)
    return (values - average) * lax.rsqrt(spread + 1e-05) * gains[0] + gains[1]


def layer_back(values, gains, delta):
    average = jnp.mean(values, axis=-1, keepdims=True)
    spread = jnp.mean(jnp.square(values - average), axis=-1, keepdims=True)
    scale = lax.rsqrt(spread + 1e-05)
    normal = (values - average) * scale
    scaled = delta * gains[0]
    result = scale * (
        scaled
        - jnp.mean(scaled, axis=-1, keepdims=True)
        - normal * jnp.mean(scaled * normal, axis=-1, keepdims=True)
    )
    return (
        result,
        jnp.sum(delta * normal, axis=(0, 1)),
        jnp.sum(delta, axis=(0, 1)),
    )


def conv(image, kernel):
    samples = image.shape[0]
    result = lax.conv_general_dilated(
        image.reshape(samples, SIDE, SIDE, -1),
        kernel.reshape(3, 3, C, C),
        (1, 1),
        ((1, 1), (1, 1)),
        dimension_numbers=("NHWC", "HWIO", "NHWC"),
        preferred_element_type=jnp.float32,
    )
    return result.reshape(samples, SIDE * SIDE, C)


def conv_back(delta, kernel):
    samples = delta.shape[0]
    result = lax.conv_general_dilated(
        delta.reshape(samples, SIDE, SIDE, -1),
        kernel.reshape(3, 3, C, C)[::-1, ::-1],
        (1, 1),
        ((1, 1), (1, 1)),
        dimension_numbers=("NHWC", "HWOI", "NHWC"),
        preferred_element_type=jnp.float32,
    )
    return result.reshape(samples, SIDE * SIDE, C)


def conv_gradient(image, delta):
    samples = image.shape[0]
    result = lax.conv_general_dilated(
        image.reshape(samples, SIDE, SIDE, -1),
        delta.reshape(samples, SIDE, SIDE, -1),
        (1, 1),
        ((1, 1), (1, 1)),
        dimension_numbers=("CHWN", "IHWO", "HWNC"),
        preferred_element_type=jnp.float32,
    )
    return result.reshape(9 * C, C)


def shifted_taps(image, sign):
    pixels = image.shape[-1]
    edge = SIDE + 1
    column = jnp.arange(pixels) % SIDE
    padded = jnp.pad(image, ((0, 0), (0, 0), (edge, edge)))
    pieces = []
    for tap in range(9):
        down, across = sign * (tap // 3 - 1), sign * (tap % 3 - 1)
        start = edge + SIDE * down + across
        piece = padded[:, :, start : start + pixels]
        if across == -1:
            piece = jnp.where(column >= 1, piece, jnp.zeros((), piece.dtype))
        if across == 1:
            piece = jnp.where(column < SIDE - 1, piece, jnp.zeros((), piece.dtype))
        pieces.append(piece)
    return pieces


def rows_dot(left, right):
    return lax.dot_general(
        left, right, (((0, 1), (0, 1)), ((), ())), preferred_element_type=jnp.float32
    )


def times(left, right):
    return lax.dot_general(
        left, right, (((2,), (0,)), ((), ())), preferred_element_type=jnp.float32
    )


def times_back(left, right):
    return lax.dot_general(
        left, right, (((2,), (1,)), ((), ())), preferred_element_type=jnp.float32
    )


def turned_times(left, right):
    return jnp.einsum("sdp,dc->spc", left, right, preferred_element_type=jnp.float32)


def turned_product(values, matrix):
    return jnp.einsum("spc,cd->sdp", values, matrix, preferred_element_type=jnp.float32)


def rows_total(values):
    return jnp.sum(values.astype(jnp.float32), axis=(0, 1))


def device_pass(weights, latents, noise, context, timesteps, region, mask_total):
    kernels, entry, middle, narrow, vectors, squares, crossing, widen = weights
    table = unpack(vectors.astype(jnp.float32))
    samples, channels_in, pixels = latents.shape
    words = context.shape[1]
    word_rows = -(-words // 16) * 16
    signal = jax.vmap(noise_level)(timesteps)[:, None, None]
    noise_value = noise.astype(jnp.float32)
    noised = lowered(
        jnp.sqrt(signal) * latents.astype(jnp.float32) + jnp.sqrt(1.0 - signal) * noise_value
    )
    columns_in = jnp.concatenate(shifted_taps(noised, 1), axis=1)
    hidden = turned_times(columns_in, vectors[0:36]) + table["input_bias"]
    feature = lowered(jax.vmap(lambda t: time_features(t, C)[0])(timesteps))
    first_pre = product(feature, entry) + table["time_in_bias"]
    first_low = lowered(jax.nn.silu(first_pre))
    second_pre = product(first_low, middle) + table["middle_bias"]
    second_low = lowered(jax.nn.silu(second_pre))
    embedding = product(second_low, narrow[0]) + table["time_out_bias"]
    stats_one = group_stats(hidden, 1e-05)
    act_one = lowered(jax.nn.silu(group_apply(hidden, stats_one, table["norm_one"])))
    inner_act = conv(act_one, kernels[0]) + table["block_one_bias"] + embedding[:, None, :]
    stats_two = group_stats(inner_act, 1e-05)
    act_two = lowered(jax.nn.silu(group_apply(inner_act, stats_two, table["norm_two"])))
    residual = hidden + conv(act_two, kernels[1]) + table["block_two_bias"]
    stats_three = group_stats(residual, 1e-06)
    normed = lowered(group_apply(residual, stats_three, table["norm_three"]))
    stream = times(normed, squares[6]) + table["project_in_bias"]
    lay_one = lowered(layer_norm(stream, table["layer_one"]))
    wide_query, wide_key, wide_value = (wide_columns(squares[index]) for index in range(3))
    queries = lowered(times(lay_one, wide_query))
    keys = lowered(times(lay_one, wide_key))
    values = lowered(times(lay_one, wide_value))
    attended, totals = attend(queries, keys, jnp.swapaxes(values, 1, 2), pixels)
    wide_self = wide_rows(squares[3])
    stream_two = stream + turned_times(attended, wide_self) + table["self_bias"]
    lay_two = lowered(layer_norm(stream_two, table["layer_two"]))
    wide_cross_query = wide_columns(squares[4])
    cross_query = lowered(times(lay_two, wide_cross_query))
    wide_context = jnp.pad(context, ((0, 0), (0, word_rows - words), (0, 0)))
    cross_key = lowered(times(wide_context, wide_columns(crossing[:, :C])))
    cross_value = lowered(times(wide_context, wide_columns(crossing[:, C:])))
    cross_attended, cross_totals = attend(
        cross_query, cross_key, jnp.swapaxes(cross_value, 1, 2), words
    )
    wide_cross = wide_rows(squares[5])
    stream_three = stream_two + turned_times(cross_attended, wide_cross) + table["cross_bias"]
    lay_three = lowered(layer_norm(stream_three, table["layer_three"]))
    gated = times(lay_three, widen) + table["gate_bias"]
    halfway = gated.shape[-1] // 2
    gated_low = lowered(
        gated[..., :halfway] * jax.nn.gelu(gated[..., halfway:], approximate=False)
    )
    stream_low = lowered(stream_three + times(gated_low, narrow[1]) + table["down_bias"])
    residual_two = residual + times(stream_low, squares[7]) + table["project_out_bias"]
    stats_out = group_stats(residual_two, 1e-05)
    act_out = lowered(jax.nn.silu(group_apply(residual_two, stats_out, table["norm_out"])))
    output_kernel = vectors[36:72]
    tap_outputs = jnp.einsum(
        "kc,spc->skp", output_kernel, act_out, preferred_element_type=jnp.float32
    )
    output = table["output_bias"][None, :, None] + sum(
        shifted_taps(tap_outputs[:, 4 * tap : 4 * tap + 4], 1)[tap] for tap in range(9)
    )
    ratio = signal / (1.0 - signal)
    factor = jnp.minimum(ratio, 5.0) / ratio
    mismatch = output - noise_value
    region_value = region.astype(jnp.float32)[:, None, :]
    loss = jnp.sum(factor * region_value * mismatch * mismatch) / (4.0 * mask_total)

    coarse_output = lowered(factor * 2.0 / (4.0 * mask_total) * region_value * mismatch)
    output_columns = jnp.concatenate(shifted_taps(coarse_output, -1), axis=1)
    output_rows = jnp.einsum(
        "skp,spc->kc", output_columns, act_out, preferred_element_type=jnp.float32
    )
    delta = turned_times(output_columns, output_kernel)
    delta = silu_slope(group_apply(residual_two, stats_out, table["norm_out"]), delta)
    delta_two, out_gain, out_offset = group_back(
        residual_two, stats_out, table["norm_out"], delta
    )
    coarse_project = lowered(delta_two)
    project_out_gradient = rows_dot(stream_low, coarse_project)
    delta_stream = times_back(coarse_project, squares[7])
    coarse_down = lowered(delta_stream)
    down_gradient = rows_dot(gated_low, coarse_down)
    delta_gated = times_back(coarse_down, narrow[1])
    gate_values = gated[..., halfway:]
    normal_cdf = 0.5 * (1.0 + lax.erf(gate_values * math.sqrt(0.5)))
    normal_pdf = jnp.exp(-0.5 * gate_values * gate_values) * (1.0 / math.sqrt(2.0 * math.pi))
    coarse_gated = lowered(
        jnp.concatenate(
            [
                delta_gated * gate_values * normal_cdf,
                delta_gated * gated[..., :halfway] * (normal_cdf + gate_values * normal_pdf),
            ],
            axis=-1,
        )
    )
    widen_gradient = rows_dot(lay_three, coarse_gated)
    delta_part, three_gain, three_offset = layer_back(
        stream_three, table["layer_three"], times_back(coarse_gated, widen)
    )
    delta_stream = delta_stream + delta_part
    coarse_cross = lowered(delta_stream)
    cross_out_gradient = slim_rows(
        jnp.einsum("sdp,spc->dc", cross_attended, coarse_cross, preferred_element_type=jnp.float32)
    )
    coarse_attended = lowered(
        jnp.einsum("dc,spc->sdp", wide_cross, coarse_cross, preferred_element_type=jnp.float32)
    )
    delta_query, delta_key, delta_value = attend_back(
        cross_query,
        cross_key,
        jnp.swapaxes(cross_key, 1, 2),
        cross_value,
        coarse_attended,
        cross_totals,
        words,
    )
    cross_query_gradient = slim_columns(
        jnp.einsum("spc,sdp->cd", lay_two, delta_query, preferred_element_type=jnp.float32)
    )
    crossing_gradient = jnp.concatenate(
        [
            slim_columns(rows_dot(wide_context, delta_key)),
            slim_columns(rows_dot(wide_context, delta_value)),
        ],
        axis=1,
    )
    delta_part, two_gain, two_offset = layer_back(
        stream_two,
        table["layer_two"],
        jnp.einsum("sdp,cd->spc", delta_query, wide_cross_query, preferred_element_type=jnp.float32),
    )
    delta_stream = delta_stream + delta_part
    coarse_self = lowered(delta_stream)
    self_out_gradient = slim_rows(
        jnp.einsum("sdp,spc->dc", attended, coarse_self, preferred_element_type=jnp.float32)
    )
    coarse_attended = lowered(
        jnp.einsum("dc,spc->sdp", wide_self, coarse_self, preferred_element_type=jnp.float32)
    )
    delta_query, delta_key, delta_value = attend_back(
        queries, keys, jnp.swapaxes(keys, 1, 2), values, coarse_attended, totals, pixels
    )
    query_gradient = slim_columns(
        jnp.einsum("spc,sdp->cd", lay_one, delta_query, preferred_element_type=jnp.float32)
    )
    key_gradient = slim_columns(rows_dot(lay_one, delta_key))
    value_gradient = slim_columns(rows_dot(lay_one, delta_value))
    delta_lay = (
        jnp.einsum("sdp,cd->spc", delta_query, wide_query, preferred_element_type=jnp.float32)
        + times_back(delta_key, wide_key)
        + times_back(delta_value, wide_value)
    )
    delta_part, one_gain, one_offset = layer_back(stream, table["layer_one"], delta_lay)
    coarse_stream = lowered(delta_stream + delta_part)
    project_in_gradient = rows_dot(normed, coarse_stream)
    delta_part, norm_three_gain, norm_three_offset = group_back(
        residual, stats_three, table["norm_three"], times_back(coarse_stream, squares[6])
    )
    delta_residual = delta_two + delta_part
    coarse_block_two = lowered(delta_residual)
    kernel_two_gradient = conv_gradient(act_two, coarse_block_two)
    delta = silu_slope(
        group_apply(inner_act, stats_two, table["norm_two"]),
        conv_back(coarse_block_two, kernels[1]),
    )
    delta_inner, norm_two_gain, norm_two_offset = group_back(
        inner_act, stats_two, table["norm_two"], delta
    )
    coarse_inner = lowered(delta_inner)
    kernel_one_gradient = conv_gradient(act_one, coarse_inner)
    delta = silu_slope(
        group_apply(hidden, stats_one, table["norm_one"]), conv_back(coarse_inner, kernels[0])
    )
    delta_part, norm_one_gain, norm_one_offset = group_back(
        hidden, stats_one, table["norm_one"], delta
    )
    coarse_hidden = lowered(delta_residual + delta_part)
    input_rows = jnp.einsum(
        "skp,spc->kc", columns_in, coarse_hidden, preferred_element_type=jnp.float32
    )
    inner_total = jnp.sum(coarse_inner.astype(jnp.float32), axis=1)
    coarse_embedding = lowered(inner_total)
    coarse_second = lowered(silu_slope(second_pre, product_right(coarse_embedding, narrow[0])))
    coarse_first = lowered(silu_slope(first_pre, product_right(coarse_second, middle)))
    bias_row = jnp.pad(
        jnp.sum(coarse_output.astype(jnp.float32), axis=(0, 2)), (0, C - channels_in)
    )
    pieces = [
        input_rows,
        output_rows,
        rows_total(coarse_hidden),
        norm_one_gain,
        norm_one_offset,
        jnp.sum(inner_total, axis=0),
        column_sum(coarse_first),
        column_sum(coarse_second),
        column_sum(coarse_embedding),
        norm_two_gain,
        norm_two_offset,
        rows_total(coarse_block_two),
        norm_three_gain,
        norm_three_offset,
        rows_total(coarse_stream),
        one_gain,
        one_offset,
        rows_total(coarse_self),
        two_gain,
        two_offset,
        rows_total(coarse_cross),
        three_gain,
        three_offset,
        rows_total(coarse_gated),
        rows_total(coarse_down),
        rows_total(coarse_project),
        out_gain,
        out_offset,
        bias_row,
    ]
    vectors_gradient = jnp.concatenate([piece.reshape(-1, C) for piece in pieces], axis=0)
    squares_gradient = [
        query_gradient,
        key_gradient,
        value_gradient,
        self_out_gradient,
        cross_query_gradient,
        cross_out_gradient,
        project_in_gradient,
        project_out_gradient,
    ]
    factors = jnp.concatenate([feature, first_low, second_low], axis=1)
    deltas = jnp.concatenate([coarse_first, coarse_second, coarse_embedding], axis=1)
    return (
        loss,
        (kernel_one_gradient, kernel_two_gradient),
        down_gradient,
        crossing_gradient,
        widen_gradient,
        vectors_gradient,
        squares_gradient,
        factors,
        deltas,
    )


def adam(weight, first, second, gradient, rate, fix_one, fix_two):
    moment = beta_one * first + (1.0 - beta_one) * gradient
    variance = beta_two * second + (1.0 - beta_two) * gradient * gradient
    update = moment / fix_one / (jnp.sqrt(variance / fix_two) + adam_eps)
    return (weight - rate * (update + decay * weight), moment, variance)


def bit_count(size):
    return max(size.bit_length() - 1, 0)


def partner_of(position, bit):
    own = (position // (2**bit)) % 2
    return own, position + (1 - 2 * own) * (2**bit)


def greet(row_index, column_index, row_bits, column_parts):
    barrier = pltpu.get_barrier_semaphore()
    for bit in range(row_bits):
        other = partner_of(row_index, bit)[1]
        pl.semaphore_signal(
            barrier, inc=1, device_id=(other, column_index), device_id_type=pl.DeviceIdType.MESH
        )
    for step in range(1, column_parts):
        other = lax.rem(column_index + step, column_parts)
        pl.semaphore_signal(
            barrier, inc=1, device_id=(row_index, other), device_id_type=pl.DeviceIdType.MESH
        )
    pl.semaphore_wait(barrier, row_bits + column_parts - 1)


def remote(source, target, send_sem, recv_sem, device):
    return pltpu.make_async_remote_copy(
        src_ref=source,
        dst_ref=target,
        send_sem=send_sem,
        recv_sem=recv_sem,
        device_id=device,
        device_id_type=pl.DeviceIdType.MESH,
    )


def add_tiles(target, own, arrived):
    lead = target.shape[:-2]
    total = math.prod(lead)

    def one(index, carry):
        coords = []
        for extent in reversed(lead):
            coords.append(lax.rem(index, extent))
            index = index // extent
        coords = tuple(reversed(coords))
        summed = own[coords].astype(jnp.float32) + arrived[coords].astype(jnp.float32)
        target[coords] = summed.astype(target.dtype)
        return carry

    if total == 1:
        zeros = (0,) * len(lead)
        summed = own[zeros].astype(jnp.float32) + arrived[zeros].astype(jnp.float32)
        target[zeros] = summed.astype(target.dtype)
    else:
        lax.fori_loop(0, total, one, 0)


def reduce_kernel(plan, row_bits, column_parts, *refs):
    count = len(plan)
    owners_ref = refs[0]
    inputs = refs[1 : count + 1]
    factor_in = refs[count + 1]
    outputs = refs[count + 2 : 2 * count + 2]
    factor_out = refs[2 * count + 2]
    scratch = list(refs[2 * count + 3 :])
    factor_send, factor_recv = scratch.pop(), scratch.pop()
    send_sems, recv_sems = scratch.pop(), scratch.pop()
    arrived, summed, outgoing, incoming = [], [], [], []
    for _ in plan:
        arrived.append([scratch.pop(0) for _ in range(row_bits)])
        summed.append([scratch.pop(0) for _ in range(row_bits)])
        outgoing.append(scratch.pop(0))
        incoming.append(scratch.pop(0))
    row_index = lax.axis_index("dp")
    column_index = lax.axis_index("fsdp")
    orders = [
        list(range(row_bits)) if forward else [0] + list(range(row_bits - 1, 0, -1))
        for _, forward in plan
    ]
    every = slice(None)

    def halves(array, stage):
        order = orders[array]
        remaining = [bit for bit in range(row_bits - 1, -1, -1) if bit not in order[:stage]]
        source = inputs[array] if stage == 0 else summed[array][stage - 1]
        axis = plan[array][0] + remaining.index(order[stage])
        own, other = partner_of(row_index, order[stage])
        kept = source.at[(every,) * axis + (own,)]
        given = source.at[(every,) * axis + (1 - own,)]
        return kept, given, other

    def swap(array, stage):
        given, other = halves(array, stage)[1:]
        return remote(
            given,
            arrived[array][stage],
            send_sems.at[array, stage],
            recv_sems.at[array, stage],
            (other, column_index),
        )

    def spread(array, step, receiving):
        other = lax.rem(column_index + step, column_parts)
        slot = other if receiving else column_index
        return remote(
            outgoing[array].at[other],
            incoming[array].at[slot],
            send_sems.at[array, row_bits + other],
            recv_sems.at[array, row_bits + slot],
            (row_index, other),
        )

    own_bits = [partner_of(row_index, bit)[0] for bit in range(row_bits - 1, -1, -1)]

    def factor_swap(stage):
        known = (column_index,) + tuple(own_bits[: row_bits - stage])
        return remote(
            factor_out.at[known],
            factor_out.at[known],
            factor_send.at[stage],
            factor_recv.at[stage],
            (partner_of(row_index, stage)[1], column_index),
        )

    def factor_arrival(stage):
        other_bits = own_bits[: row_bits - stage - 1] + [1 - own_bits[row_bits - stage - 1]]
        there = (column_index,) + tuple(other_bits)
        return remote(
            factor_out.at[there],
            factor_out.at[there],
            factor_send.at[stage],
            factor_recv.at[stage],
            (partner_of(row_index, stage)[1], column_index),
        )

    def factor_spread(step, receiving):
        other = lax.rem(column_index + step, column_parts)
        slot = other if receiving else column_index
        return remote(
            factor_out.at[slot],
            factor_out.at[slot],
            factor_send.at[row_bits + other],
            factor_recv.at[row_bits + slot],
            (row_index, other),
        )

    factor_out[(column_index,) + tuple(own_bits)] = factor_in[...]
    greet(row_index, column_index, row_bits, column_parts)
    for array in range(count):
        swap(array, 0).start()
    factor_swap(0).start()
    for stage in range(row_bits):
        for array in range(count):
            copy = swap(array, stage)
            copy.wait_recv()
            copy.wait_send()
            add_tiles(summed[array][stage], halves(array, stage)[0], arrived[array][stage])
            if stage + 1 < row_bits:
                swap(array, stage + 1).start()
                continue
            result = summed[array][stage]
            prefix = plan[array][0]
            parts = outgoing[array]
            for column in range(column_parts):
                if prefix:
                    held = parts.shape[1]
                    for place in range(held):
                        parts[column, place] = result[owners_ref[column * held + place]]
                else:
                    width = parts.shape[-1]
                    parts[column] = result[:, column * width : (column + 1) * width]
            for step in range(1, column_parts):
                spread(array, step, False).start()
        factor_arrival(stage).wait_recv()
        factor_swap(stage).wait_send()
        if stage + 1 < row_bits:
            factor_swap(stage + 1).start()
        else:
            for step in range(1, column_parts):
                factor_spread(step, False).start()
    for array in range(count):
        total = outgoing[array][column_index].astype(jnp.float32)
        for step in range(1, column_parts):
            spread(array, step, True).wait_recv()
            slot = lax.rem(column_index + step, column_parts)
            total = total + incoming[array][slot].astype(jnp.float32)
        outputs[array][...] = total
        for step in range(1, column_parts):
            spread(array, step, False).wait_send()
    for step in range(1, column_parts):
        factor_spread(step, True).wait_recv()
        factor_spread(step, False).wait_send()


def reduce_all(arrays, prefixes, forwards, factors, owners, row_parts, column_parts):
    row_bits = bit_count(row_parts)
    plan = list(zip(prefixes, forwards))
    vmem = pl.BlockSpec(memory_space=pltpu.VMEM)
    scratch, shapes = [], []
    for value, prefix in zip(arrays, prefixes):
        lead, tail = value.shape[:prefix], value.shape[-2:]
        stages = [lead + (2,) * (row_bits - 1 - stage) + tail for stage in range(row_bits)]
        scratch += [pltpu.VMEM(shape, jnp.bfloat16) for shape in stages] * 2
        if prefix:
            part = (lead[0] // column_parts,) + tail
        else:
            part = (tail[0], tail[1] // column_parts)
        scratch += [pltpu.VMEM((column_parts,) + part, jnp.bfloat16)] * 2
        shapes.append(jax.ShapeDtypeStruct(part, jnp.float32))
    shapes.append(
        jax.ShapeDtypeStruct(
            (column_parts,) + (2,) * row_bits + factors.shape, factors.dtype
        )
    )
    count = len(arrays)
    scratch += [
        pltpu.SemaphoreType.DMA((count, row_bits + column_parts)),
        pltpu.SemaphoreType.DMA((count, row_bits + column_parts)),
        pltpu.SemaphoreType.DMA((row_bits + column_parts,)),
        pltpu.SemaphoreType.DMA((row_bits + column_parts,)),
    ]
    return pl.pallas_call(
        partial(reduce_kernel, plan, row_bits, column_parts),
        in_specs=[pl.BlockSpec(memory_space=pltpu.SMEM)] + [vmem] * (count + 1),
        out_specs=[vmem] * (count + 1),
        out_shape=shapes,
        scratch_shapes=scratch,
        compiler_params=pltpu.CompilerParams(
            collective_id=1, has_side_effects=True, vmem_limit_bytes=60 * 1024 * 1024
        ),
        name="reduce_all",
    )(owners, *arrays, factors)


BLOCK = 64


def exact(left, right, left_dim, right_dim):
    return lax.dot_general(
        left,
        right,
        (((left_dim,), (right_dim,)), ((), ())),
        precision=highest,
        preferred_element_type=jnp.float32,
    )


def soap_kernel(
    row_bits,
    column_parts,
    scalars_ref,
    part_ref,
    state_ref,
    grad_ref,
    bases_ref,
    returned_ref,
    totals_ref,
    work,
    small,
    shared,
    direction,
    turned_ref,
    number_send,
    number_recv,
    outgoing,
    number_sems,
    shared_sems,
    return_sems,
):
    held, rows, size = part_ref.shape
    row_parts = 2**row_bits
    column_bits = bit_count(column_parts)
    row_index = lax.axis_index("dp")
    column_index = lax.axis_index("fsdp")
    fix_one, fix_two = scalars_ref[2], scalars_ref[3]
    own_bits = [partner_of(row_index, bit)[0] for bit in range(row_bits - 1, -1, -1)]
    every = slice(None)
    shared[(every,) + tuple(own_bits)] = part_ref[...]
    tile_lane = lax.broadcasted_iota(jnp.int32, (8, 128), 1)
    numbers = jnp.where(
        tile_lane == 0, scalars_ref[0], jnp.where(tile_lane == 1, scalars_ref[1], 0.0)
    )
    number_send[0] = numbers
    greet(row_index, column_index, row_bits, column_parts)

    def number_swap(stage):
        if stage < row_bits:
            device = (partner_of(row_index, stage)[1], column_index)
        else:
            device = (row_index, partner_of(column_index, stage - row_bits)[1])
        return remote(
            number_send.at[stage],
            number_recv.at[stage],
            number_sems.at[0, stage],
            number_sems.at[1, stage],
            device,
        )

    def shared_swap(stage, arriving):
        known = own_bits[: row_bits - stage]
        if arriving:
            known = known[:-1] + [1 - known[-1]]
        place = shared.at[(every,) + tuple(known)]
        device = (partner_of(row_index, stage)[1], column_index)
        return remote(place, place, shared_sems.at[0, stage], shared_sems.at[1, stage], device)

    def early(slot, carry):
        left_basis, right_basis = state_ref[4, slot], state_ref[5, slot]
        turned_ref[slot] = exact(
            exact(left_basis, state_ref[0, slot], 0, 0), right_basis, 1, 0
        )
        work[2 * slot, :, size : 2 * size] = exact(left_basis, state_ref[2, slot], 0, 1)
        work[2 * slot + 1, :, size : 2 * size] = exact(right_basis, state_ref[3, slot], 0, 1)
        return carry

    number_swap(0).start()
    shared_swap(0, False).start()
    rounds = row_bits + column_bits
    for stage in range(rounds):
        if stage < held:
            early(stage, 0)
        number_swap(stage).wait()
        numbers = numbers + number_recv[stage]
        if stage + 1 < rounds:
            number_send[stage + 1] = numbers
        if stage < row_bits:
            shared_swap(stage, True).wait_recv()
            shared_swap(stage, False).wait_send()
            if stage + 1 < row_bits:
                shared_swap(stage + 1, False).start()
        if stage + 1 < rounds:
            number_swap(stage + 1).start()
    totals_ref[...] = numbers
    for slot in range(held):
        for place in range(row_parts):
            bits = tuple((place >> bit) & 1 for bit in range(row_bits - 1, -1, -1))
            grad_ref[slot, place * rows : (place + 1) * rows] = shared[(slot,) + bits]
    norm = jnp.sqrt(numbers[0:1, 0:1])
    clip = jnp.minimum(1.0, clip_limit / norm)

    def prepare(slot, carry):
        gradient = grad_ref[slot] * clip
        grad_ref[slot] = gradient
        left_basis, right_basis = state_ref[4, slot], state_ref[5, slot]
        left_turned = exact(left_basis, gradient, 0, 0)
        right_turned = exact(gradient, right_basis, 1, 0)
        rotated = exact(left_turned, right_basis, 1, 0)
        second = beta_two * state_ref[1, slot] + (1.0 - beta_two) * rotated * rotated
        turned_moment = beta_one * turned_ref[slot] + (1.0 - beta_one) * rotated
        scaled = turned_moment / fix_one / (jnp.sqrt(second / fix_two) + adam_eps)
        direction[slot] = exact(exact(left_basis, scaled, 1, 0), right_basis, 1, 1)
        for side in range(2):
            if side == 0:
                outer = exact(left_turned, gradient, 1, 1)
            else:
                outer = exact(right_turned, gradient, 0, 0)
            place = 2 * slot + side
            image = beta_stat * work[place, :, size : 2 * size] + (1.0 - beta_stat) * outer
            work[place, :, size : 2 * size] = image
            work[place, :, 0:size] = exact(image, image, 1, 1)
        return carry

    lax.fori_loop(0, held, prepare, 0)
    width = size // column_parts
    for slot in range(held):
        mine = jnp.zeros((rows, size), jnp.float32)
        for place in range(row_parts):
            mine = jnp.where(
                row_index == place, direction[slot, place * rows : (place + 1) * rows], mine
            )
        for column in range(column_parts):
            outgoing[column, slot] = mine[:, column * width : (column + 1) * width]

    def give_back(step, receiving):
        other = lax.rem(column_index + step, column_parts)
        slot = other if receiving else column_index
        return remote(
            outgoing.at[other],
            returned_ref.at[slot],
            return_sems.at[0, other],
            return_sems.at[1, slot],
            (row_index, other),
        )

    returned_ref[column_index] = outgoing[column_index]
    for step in range(1, column_parts):
        give_back(step, False).start()
    count = 2 * held
    row = lax.broadcasted_iota(jnp.int32, (BLOCK, 2 * BLOCK), 0)
    lane = lax.broadcasted_iota(jnp.int32, (BLOCK, 2 * BLOCK), 1)
    unit = jnp.where(lane == row + BLOCK, 1.0, 0.0)
    lane_row = lax.broadcasted_iota(jnp.int32, (1, 2 * BLOCK), 1)
    for block in range(size // BLOCK):
        top = block * BLOCK
        for index in range(count):
            diagonal = work[index, top : top + BLOCK, top : top + BLOCK]
            small[index] = unit + jnp.concatenate(
                [diagonal, jnp.zeros((BLOCK, BLOCK), jnp.float32)], axis=1
            )

        def eliminate(half, carry):
            step = 2 * half
            matrices = [small[index] for index in range(count)]
            pairs = [
                (small[index, pl.ds(step, 1), :], small[index, pl.ds(step + 1, 1), :])
                for index in range(count)
            ]
            results = []
            for matrix, (row_one, row_two) in zip(matrices, pairs):
                column_one = jnp.sum(
                    jnp.where(lane == step, matrix, 0.0), axis=1, keepdims=True
                )
                column_two = jnp.sum(
                    jnp.where(lane == step + 1, matrix, 0.0), axis=1, keepdims=True
                )
                corner = jnp.sum(
                    jnp.where(lane_row == step, row_one, 0.0), axis=1, keepdims=True
                )
                cross = jnp.sum(
                    jnp.where(lane_row == step + 1, row_one, 0.0), axis=1, keepdims=True
                )
                last = jnp.sum(
                    jnp.where(lane_row == step + 1, row_two, 0.0), axis=1, keepdims=True
                )
                scale_one = lax.rsqrt(corner)
                slope = cross * scale_one * scale_one
                scale_two = lax.rsqrt(last - slope * cross)
                kept_one = row_one * scale_one
                kept_two = (row_two - slope * row_one) * scale_two
                ratio_one = column_one * scale_one
                ratio_two = (column_two - slope * column_one) * scale_two
                results.append(
                    jnp.where(
                        row > step + 1,
                        matrix - ratio_one * kept_one - ratio_two * kept_two,
                        jnp.where(
                            row == step, kept_one, jnp.where(row == step + 1, kept_two, matrix)
                        ),
                    )
                )
            for index in range(count):
                small[index] = results[index]
            return carry

        lax.fori_loop(0, BLOCK // 2, eliminate, 0)

        def sweep(index, carry):
            inverse = small[index][:, BLOCK : 2 * BLOCK]
            panel = exact(inverse, work[index, top : top + BLOCK, :], 1, 0)
            work[index, top : top + BLOCK, :] = panel
            if top + BLOCK < size:
                lower_part = exact(panel[:, top + BLOCK : size], panel, 0, 0)
                work[index, top + BLOCK : size, :] = (
                    work[index, top + BLOCK : size, :] - lower_part
                )
            return carry

        lax.fori_loop(0, count, sweep, 0)

    def finish(slot, carry):
        for side in range(2):
            bases_ref[side, slot] = work[2 * slot + side, :, size : 2 * size].T
        return carry

    lax.fori_loop(0, held, finish, 0)
    for step in range(1, column_parts):
        give_back(step, True).wait_recv()
        give_back(step, False).wait_send()


def soap_apply(scalars, part, state, row_parts, column_parts):
    held, rows, size = part.shape
    row_bits = bit_count(row_parts)
    rounds = row_bits + bit_count(column_parts)
    square = (held, size, size)
    f32 = jnp.float32
    vmem = pl.BlockSpec(memory_space=pltpu.VMEM)
    moved = (column_parts, held, rows, size // column_parts)
    return pl.pallas_call(
        partial(soap_kernel, row_bits, column_parts),
        in_specs=[pl.BlockSpec(memory_space=pltpu.SMEM), vmem, vmem],
        out_specs=[vmem] * 4,
        out_shape=[
            jax.ShapeDtypeStruct(square, f32),
            jax.ShapeDtypeStruct((2,) + square, f32),
            jax.ShapeDtypeStruct(moved, f32),
            jax.ShapeDtypeStruct((8, 128), f32),
        ],
        scratch_shapes=[
            pltpu.VMEM((2 * held, size, 2 * size), f32),
            pltpu.VMEM((2 * held, BLOCK, 2 * BLOCK), f32),
            pltpu.VMEM((held,) + (2,) * row_bits + (rows, size), f32),
            pltpu.VMEM(square, f32),
            pltpu.VMEM(square, f32),
            pltpu.VMEM((rounds, 8, 128), f32),
            pltpu.VMEM((rounds, 8, 128), f32),
            pltpu.VMEM(moved, f32),
            pltpu.SemaphoreType.DMA((2, rounds)),
            pltpu.SemaphoreType.DMA((2, row_bits)),
            pltpu.SemaphoreType.DMA((2, column_parts)),
        ],
        compiler_params=pltpu.CompilerParams(
            collective_id=2, has_side_effects=True, vmem_limit_bytes=60 * 1024 * 1024
        ),
        name="soap",
    )(scalars, part, state)


def assemble(pieces, row_parts, column_parts):
    height, breadth = pieces.shape[-2:]
    shaped = pieces.reshape(row_parts, column_parts, height, breadth)
    return shaped.transpose(0, 2, 1, 3).reshape(row_parts * height, column_parts * breadth)


def on_device(
    latents,
    noise,
    context,
    timesteps,
    region_mask,
    owners,
    step_count,
    kernels_weight,
    kernels_first,
    kernels_second,
    entry_weight,
    entry_first,
    entry_second,
    middle_weight,
    middle_first,
    middle_second,
    narrow_weight,
    narrow_first,
    narrow_second,
    crossing_weight,
    crossing_first,
    crossing_second,
    widen_weight,
    widen_first,
    widen_second,
    vectors_weight,
    vectors_first,
    vectors_second,
    squares_weight,
    squares_state,
):
    axes = ("dp", "fsdp")
    row_parts = lax.axis_size("dp")
    column_parts = lax.axis_size("fsdp")
    row_index = lax.axis_index("dp")
    column_index = lax.axis_index("fsdp")
    slots = owners.shape[0]

    def gather(value):
        return lax.all_gather(value[None], axes, axis=0, tiled=True)

    def whole(pieces):
        return assemble(pieces, row_parts, column_parts)

    kernel_rows = kernels_weight.shape[1]
    narrow_rows = narrow_weight.shape[1]
    vector_rows = vectors_weight.shape[0]
    square_rows = squares_weight.shape[1]
    tall = [
        kernels_weight[0],
        kernels_weight[1],
        narrow_weight[0],
        narrow_weight[1],
        vectors_weight,
    ] + [squares_weight[index] for index in range(slots)]
    sizes = [piece.shape[0] for piece in tall]
    tall_all = gather(jnp.concatenate([lowered(piece) for piece in tall], axis=0))
    starts = [sum(sizes[:index]) for index in range(len(sizes))]
    tall_full = [
        whole(tall_all[:, start : start + size]) for start, size in zip(starts, sizes)
    ]
    even_all = gather(jnp.concatenate([lowered(entry_weight), lowered(middle_weight)], axis=0))
    entry_rows = entry_weight.shape[0]
    weights = (
        tall_full[0:2],
        whole(even_all[:, :entry_rows]),
        whole(even_all[:, entry_rows:]),
        tall_full[2:4],
        tall_full[4],
        tall_full[5:],
        whole(gather(lowered(crossing_weight))),
        whole(gather(lowered(widen_weight))),
    )
    mask_total = lax.psum(jnp.sum(region_mask.astype(jnp.float32)), axes)
    merged = [
        value.reshape((value.shape[0] * value.shape[1],) + value.shape[2:])
        for value in (latents, noise, context, timesteps, region_mask)
    ]
    loss, kernel_grads, down, crossing, widen, vectors, squares, factors, deltas = device_pass(
        weights, *merged, mask_total
    )
    steps = step_count[0].astype(jnp.float32)
    fix_one = 1.0 - jnp.power(jnp.float32(beta_one), steps)
    fix_two = 1.0 - jnp.power(jnp.float32(beta_two), steps)
    row_bits = bit_count(row_parts)
    halves = (2,) * row_bits
    factor_rows = -(-2 * factors.size // LANES // 16) * 16

    def blocks(value):
        value = lowered(value)
        return value.reshape(halves + (value.shape[0] // row_parts, value.shape[1]))

    vector_blocks = jnp.pad(
        lowered(vectors).reshape(row_parts, vector_rows, C),
        ((0, 0), (0, -vector_rows % 16), (0, 0)),
    )
    packed = jnp.concatenate([factors.reshape(-1), deltas.reshape(-1)])
    packed = jnp.pad(packed, (0, factor_rows * LANES - packed.size)).reshape(factor_rows, LANES)
    (
        kernel_one_part,
        kernel_two_part,
        squares_part,
        widen_part,
        down_part,
        crossing_part,
        vectors_part,
        all_factors,
    ) = reduce_all(
        [
            blocks(kernel_grads[0]),
            blocks(kernel_grads[1]),
            jnp.stack([blocks(piece) for piece in squares]),
            blocks(widen),
            blocks(down),
            blocks(crossing),
            vector_blocks.reshape(halves + vector_blocks.shape[1:]),
        ],
        [0, 0, 1, 0, 0, 0, 0],
        [True, False, True, False, True, False, False],
        packed,
        owners,
        row_parts,
        column_parts,
    )
    gathered = all_factors.reshape(row_parts * column_parts, factor_rows * LANES)
    all_deltas = gathered[:, factors.size : 2 * factors.size].reshape(-1, deltas.shape[1])
    all_factors = gathered[:, : factors.size].reshape(-1, factors.shape[1])

    def outer(row_start, rows, column_start, columns):
        left = lax.dynamic_slice_in_dim(all_factors, row_start + row_index * rows, rows, 1)
        right = lax.dynamic_slice_in_dim(
            all_deltas, column_start + column_index * columns, columns, 1
        )
        return product_left(left, right)

    entry_part = outer(0, entry_weight.shape[0], 0, entry_weight.shape[1])
    middle_part = outer(C, middle_weight.shape[0], 4 * C, middle_weight.shape[1])
    time_part = outer(5 * C, narrow_rows, 8 * C, narrow_weight.shape[2])
    kernels_part = jnp.stack([kernel_one_part, kernel_two_part])
    narrow_part = jnp.stack([time_part, down_part])
    vectors_part = vectors_part[:vector_rows]
    parts = (
        kernels_part,
        entry_part,
        middle_part,
        narrow_part,
        crossing_part,
        widen_part,
        vectors_part,
        squares_part,
    )
    local_square = sum((jnp.sum(piece * piece) for piece in parts))
    squares_grad, squares_slots, returned, both = soap_apply(
        jnp.stack([local_square, loss, fix_one, fix_two]),
        squares_part,
        squares_state,
        row_parts,
        column_parts,
    )
    grad_norm = jnp.sqrt(both[0, 0])
    loss = both[0, 1]
    clip = jnp.minimum(1.0, clip_limit / grad_norm)
    returned = returned.reshape((slots,) + returned.shape[2:])
    picker = (owners[:, None] == jnp.arange(slots)[None, :]).astype(jnp.float32)
    direction_shard = jnp.einsum("sm,sab->mab", picker, returned, precision=highest)
    rate_list = rates()
    squares_master = squares_weight - rate_list[7] * (direction_shard + decay * squares_weight)
    results = []
    for index, (weight, first, second) in enumerate(
        (
            (kernels_weight, kernels_first, kernels_second),
            (entry_weight, entry_first, entry_second),
            (middle_weight, middle_first, middle_second),
            (narrow_weight, narrow_first, narrow_second),
            (crossing_weight, crossing_first, crossing_second),
            (widen_weight, widen_first, widen_second),
            (vectors_weight, vectors_first, vectors_second),
        )
    ):
        results.extend(
            adam(weight, first, second, parts[index] * clip, rate_list[index], fix_one, fix_two)
        )
    totals = jnp.stack([loss, grad_norm])
    return (totals, *results, squares_master, squares_slots, squares_grad)


def solution(mesh):
    return jax.shard_map(
        on_device,
        mesh=mesh,
        in_specs=(
            P(None, ("dp", "fsdp"), None, None),
            P(None, ("dp", "fsdp"), None, None),
            P(None, ("dp", "fsdp"), None, None),
            P(None, ("dp", "fsdp")),
            P(None, ("dp", "fsdp"), None),
            P(),
            P(),
            P(None, "dp", "fsdp"),
            P(None, "dp", "fsdp"),
            P(None, "dp", "fsdp"),
            P("dp", "fsdp"),
            P("dp", "fsdp"),
            P("dp", "fsdp"),
            P("dp", "fsdp"),
            P("dp", "fsdp"),
            P("dp", "fsdp"),
            P(None, "dp", "fsdp"),
            P(None, "dp", "fsdp"),
            P(None, "dp", "fsdp"),
            P("dp", "fsdp"),
            P("dp", "fsdp"),
            P("dp", "fsdp"),
            P("dp", "fsdp"),
            P("dp", "fsdp"),
            P("dp", "fsdp"),
            P("dp", "fsdp"),
            P("dp", "fsdp"),
            P("dp", "fsdp"),
            P(None, "dp", "fsdp"),
            P(None, "fsdp", None, None),
        ),
        out_specs=(
            P(),
            P(None, "dp", "fsdp"),
            P(None, "dp", "fsdp"),
            P(None, "dp", "fsdp"),
            P("dp", "fsdp"),
            P("dp", "fsdp"),
            P("dp", "fsdp"),
            P("dp", "fsdp"),
            P("dp", "fsdp"),
            P("dp", "fsdp"),
            P(None, "dp", "fsdp"),
            P(None, "dp", "fsdp"),
            P(None, "dp", "fsdp"),
            P("dp", "fsdp"),
            P("dp", "fsdp"),
            P("dp", "fsdp"),
            P("dp", "fsdp"),
            P("dp", "fsdp"),
            P("dp", "fsdp"),
            P("dp", "fsdp"),
            P("dp", "fsdp"),
            P("dp", "fsdp"),
            P(None, "dp", "fsdp"),
            P(None, "fsdp", None, None),
            P("fsdp", None, None),
        ),
        check_vma=False,
    )
```

time: 4010 us -> 1190 us (0.30)
  local copies, waits for them, and re-layouts: 1260 us -> 236 us
  waiting for transfers between devices: 982 us -> 32.1 us
  other arithmetic: 632 us -> 110 us
  blocking collectives: 550 us -> 129 us
  Pallas kernels: 0 us -> 395 us
  matrix products: 511 us -> 251 us
    reduce_scatter x5 -> x0, waiting for transfers between devices: 689 us -> none  [the longest x1 154 us: on_device(): lax.psum_scatter(spread[3], ('dp', 'fsdp'), scatter_dimension=0, tiled=True)]
    scatter-add x42 -> x0, local copies, waits for them, and re-layouts: 527 us -> none  [fold_back(): folded.at[row_offset:row_offset + SIDE, col_offset:col_offset + SIDE]]
    pallas_call x0 -> x6, Pallas kernels: none -> 395 us  [the longest x2 108 us: attend_back(): pl.pallas_call(partial(attend_back_kernel, valid), grid=(samples, wide //...]
    all_gather x7 -> x1, blocking collectives: 468 us -> 86.4 us  [gather(): return lax.all_gather(value[None], axes, axis=0, tiled=True)]
    another operation x66 -> x6, other arithmetic: 360 us -> 3.23 us  [the longest x21 197 us: orthonormal(): cholesky_factor = jnp.linalg.cholesky(gram_matrix)]
    unnamed x11 -> x3, waiting for transfers between devices: 286 us -> 0.05 us
    slice x96 -> x62, local copies, waits for them, and re-layouts: 265 us -> 62.5 us  [the longest x4 14.9 us: on_device(): tall_all[:, start:start + size]]
    dot_general x35 -> x55, matrix products: 291 us -> 90.1 us  [the longest x6 28.6 us: times_back(): lax.dot_general(left, right, (((2,), (1,)), ((), ())), preferred_element_...]
  transfers between devices with their start and end apart: 20 -> 3, of which waited for: 8 -> 1; matrix products, arithmetic and copies ran while one was open for 16% -> 4% of each run, Pallas kernels for 0% -> 0%
where the time goes in v1:
time: 1190 us; the launch traced here: 1180 us
  Pallas kernels  395 us (33%)
  matrix products  251 us (21%)
  local copies, waits for them, and re-layouts  236 us (20%)
  blocking collectives  129 us (11%)
  other arithmetic  110 us (9%)
  waiting for transfers between devices  32.1 us (3%)
  between operations  25.2 us (2%)
    pallas_call x2, Pallas kernels, attend_back(): pl.pallas_call(partial(attend_back_kernel, valid), grid=(samples, wide //...  108 us
    pallas_call x1, Pallas kernels, soap_apply(): pl.pallas_call(partial(soap_kernel, row_bits, column_parts), in_specs=[pl...  101 us
    pallas_call x1, Pallas kernels, reduce_all(): pl.pallas_call(partial(reduce_kernel, plan, row_bits, column_parts), in_s...  96.4 us
    pallas_call x2, Pallas kernels, attend(): pl.pallas_call(partial(attend_kernel, valid), grid=(samples, wide // LANE...  89.3 us
    all_gather x1, blocking collectives, gather(): return lax.all_gather(value[None], axes, axis=0, tiled=True)  86.4 us
    conv_general_dilated x2, matrix products, conv_back(): lax.conv_general_dilated(delta.reshape(samples, SIDE, SIDE, -1), kernel.r...  60.8 us
    conv_general_dilated x2, matrix products, conv_gradient(): lax.conv_general_dilated(image.reshape(samples, SIDE, SIDE, -1), delta.re...  50.5 us
    psum x1, blocking collectives, on_device(): mask_total = lax.psum(jnp.sum(region_mask.astype(jnp.float32)), axes)  42.3 us
  transfers between devices with their start and end apart: 3, of which 1 were waited for; matrix products, arithmetic and copies ran while one was open for 4% of the time, Pallas kernels for 0%

profile of v1, /device:TPU:0, one launch (start us, length us, event | category | flops | bytes accessed | tf_op | source)
XLA Modules:
  0.0 1178.2 jit_solution(11553966370010600772)
XLA Ops:
  17.2 42.3 %psum.7 = f32[]{:T(128)} all-reduce(f32[]{:T(128)} %convert_reduce_fusion), channel_id=1, replica_groups=mesh['dp'=8,'fsdp'=4] {'dp','fsdp'}, use_global_device_ids=true, to_apply=%region_18.19 | all-reduce | flops 1 | bytes 8 | tf_op jit(solution)/shard_map/psum | solution.py:1281
  66.2 86.4 %all-gather.5 = bf16[32,96,160]{1,2,0:T(8,128)(2,1)S(1)} all-gather(bf16[1,96,160]{1,2,0:T(8,128)(2,1)S(1)} %convert_bitcast_fusion), channel_id=4, replica_groups=mesh['dp'=8,'fsdp'=4] {'dp','fsdp'}, dimensions={0}, use_global_device_ids=true | all-gather | bytes 1013760 | tf_op jit(solution)/shard_map/all_gather | solution.py:1247
  158.2 3.2 concatenate.151
  163.4 2.1 copy.628
  168.4 2.7 slice.731
  171.1 4.0 copy.505
  175.1 7.8 reshape.784
  184.0 32.1 %all-gather.14.cloned.1.call-done = bf16[32,1374,80]{1,2,0:T(8,128)(2,1)} async-done(((bf16[1,1374,80]{1,2,0:T(8,128)(2,1)}), bf16[32,1374,80]{1,2,0:T(8,128)(2,1)}) %all-gather.14.cloned.1.call-update) | async-done | bytes 7034896 | tf_op jit(solution)/shard_map/all_gather | solution.py:1247
  219.8 6.5 fusion.416
  255.2 3.1 multiply_convert_fusion.6
  258.9 3.5 fusion.417
  264.2 3.2 reshape.874
  268.2 2.4 reshape.786
  273.3 2.3 multiply_convert_fusion.4
  275.6 2.6 copy.500
  278.2 3.5 fusion.418
  281.7 2.5 copy.626
  284.2 2.4 copy.627
  297.0 8.1 reshape_reshape.8
  305.1 7.1 copy.503
  312.1 8.1 reshape_reshape.9
  320.3 7.1 copy.508
  328.8 20.2 %fusion.241 = (f32[2,320]{1,0:T(2,128)S(1)}, f32[2,32,32,320]{3,0,2,1:T(2,128)S(1)}) fusion(f32[2,320]{1,0:T(2,128)S(1)} %convolution_add_fusion.3, f32[320]{0:T(512)S(1)} %copy-done.167, bf16[3,3,320,320]{3,2,1,0:T(8,128)(2,1)} %copy.503, bf16[2,32,32,320]{3,2,1,0:T(8,128)(2,1)} %bitcast.417), kind=kOutput, calls=%fused_computation.340 | convolution fusion | flops 3621191168 | bytes 5781760 | tf_op jit(solution)/shard_map/conv_general_dilated | solution.py:354
  349.4 2.7 multiply_reduce_fusion
  352.4 5.0 multiply_convert_fusion.2
  357.4 16.5 %fusion.440 = f32[2,32,32,320]{3,0,2,1:T(2,128)} fusion(bf16[2,32,32,320]{3,0,2,1:T(2,128)(2,1)S(1)} %multiply_convert_fusion.2, bf16[3,3,320,320]{3,2,1,0:T(8,128)(2,1)S(1)} %copy-done.50), kind=kOutput, calls=%fused_computation.662 | convolution fusion | flops 3619225600 | bytes 5775360 | tf_op jit(solution)/shard_map/conv_general_dilated | solution.py:354
  374.0 5.9 copy.510
  379.9 2.3 fusion.415
  389.3 2.5 convolution_convert_fusion.5.v_ref
  393.0 2.6 convolution_convert_fusion.7.q_ref
  395.7 61.1 %attend.2 = (bf16[2,384,1024]{2,1,0:T(8,128)(2,1)S(1)}, f32[2,3,8,1024]{3,2,1,0:T(8,128)S(1)}) custom-call(bf16[2,1024,384]{2,1,0:T(8,128)(2,1)S(1)} %convolution_convert_fusion.7.q_ref, bf16[2,1024,384]{2,1,0:T(8,128)(2,1)S(1)} %copy-done.2, bf16[2,384,1024]{2,1,0:T(8,128)(2,1)S(1)} %copy.518.vt_ref), custom_call_target="tpu_custom_call" | custom-call | flops 8589934592 | bytes 6291456 | tf_op jit(solution)/shard_map/attend/pallas_call | solution.py:181
  461.3 28.3 %attend.3 = (bf16[2,384,1024]{2,1,0:T(8,128)(2,1)S(1)}, f32[2,3,8,1024]{3,2,1,0:T(8,128)S(1)}) custom-call(bf16[2,1024,384]{2,1,0:T(8,128)(2,1)S(1)} %convolution_convert_fusion.4.q_ref, bf16[2,80,384]{2,1,0:T(8,128)(2,1)S(1)} %copy-done.9, bf16[2,384,80]{2,1,0:T(8,128)(2,1)S(1)} %copy.532.vt_ref), custom_call_target="tpu_custom_call" | custom-call | flops 671088640 | bytes 6291456 | tf_op jit(solution)/shard_map/attend/pallas_call | solution.py:181
  490.9 2.0 copy-done.57
  492.9 6.0 broadcast_add_fusion
  498.9 23.2 %fusion.3 = bf16[2,1024,1280]{2,1,0:T(8,128)(2,1)S(1)} fusion(f32[2,1024,2560]{2,1,0:T(8,128)S(1)} %broadcast_add_fusion), kind=kLoop, calls=%fused_computation.5 | loop fusion | flops 173015040 | bytes 26214400 | tf_op jit(solution)/shard_map/convert_element_type | solution.py:29
  522.2 1.9 add_convert_fusion.2
  533.6 4.7 concatenate.163
  538.2 2.5 fusion.78
  540.8 4.6 fusion.153
  550.3 15.5 %multiply_convert_fusion = (bf16[2,1024,1280]{2,1,0:T(8,128)(2,1)}, bf16[2,1024,1280]{2,1,0:T(8,128)(2,1)}) fusion(f32[2,1024,2560]{2,1,0:T(8,128)} %copy-done.38, bf16[1280,320,1]{0,1,2:T(8,128)(2,1)S(1)} %copy-done.81, f32[2,1024,320]{1,2,0:T(8,128)S(1)} %fusion.385), kind=kOutput, calls=%fused_computation.13 | convolution fusion | flops 1715077120 | bytes 34897920 | tf_op jit(solution)/shard_map/dot_general | solution.py:422
  565.8 2.8 fusion.20
  568.6 6.2 fusion.18
  574.8 8.4 multiply_reduce_fusion.1
  583.2 9.0 fusion.17
  597.4 30.1 %attend_back.2 = (bf16[2,384,1024]{2,1,0:T(8,128)(2,1)S(1)}, bf16[2,80,384]{2,1,0:T(8,128)(2,1)S(1)}, bf16[2,80,384]{2,1,0:T(8,128)(2,1)S(1)}) custom-call(bf16[2,1024,384]{2,1,0:T(8,128)(2,1)S(1)} %copy-done.12, bf16[2,80,384]{2,1,0:T(8,128)(2,1)S(1)} %copy-done.10, bf16[2,384,80]{2,1,0:T(8,128)(2,1)S(1)} %bitcast.373, bf16[2,80,384]{2,1,0:T(8,128)(2,1)S(1)} %copy-done.7, ...), custom_call_target="tpu_custom_call" | custom-call | flops 1677721600 | bytes 12582912 | tf_op jit(solution)/shard_map/attend_back/pallas_call | solution.py:266
  632.4 2.0 multiply_reduce_fusion.2
  639.6 77.7 %attend_back.3 = (bf16[2,384,1024]{2,1,0:T(8,128)(2,1)S(1)}, bf16[2,1024,384]{2,1,0:T(8,128)(2,1)S(1)}, bf16[2,1024,384]{2,1,0:T(8,128)(2,1)S(1)}) custom-call(bf16[2,1024,384]{2,1,0:T(8,128)(2,1)S(1)} %copy-done.16, bf16[2,1024,384]{2,1,0:T(8,128)(2,1)S(1)} %copy-done.3, bf16[2,384,1024]{2,1,0:T(8,128)(2,1)S(1)} %bitcast.371, ...), custom_call_target="tpu_custom_call" | custom-call | flops 21474836480 | bytes 12582912 | tf_op jit(solution)/shard_map/attend_back/pallas_call | solution.py:266
  726.6 2.4 multiply_reduce_fusion.3
  732.5 2.1 fusion.155
  735.3 2.9 fusion.413
  739.9 25.8 %convolution_convert_fusion = bf16[3,3,320,320]{3,2,1,0:T(8,128)(2,1)} fusion(bf16[2,32,32,320]{3,0,2,1:T(2,128)(2,1)S(1)} %copy-done.60, bf16[2,32,32,320]{3,2,1,0:T(8,128)(2,1)} %bitcast.419), kind=kOutput, calls=%fused_computation.135 | convolution fusion | flops 3620147200 | bytes 4464640 | tf_op jit(solution)/shard_map/conv_general_dilated | solution.py:380
  765.8 36.0 %multiply_reduce_fusion.18 = (bf16[320]{0:T(512)(128)(2,1)}, f32[2,320]{1,0:T(2,128)S(1)}, bf16[320]{0:T(512)(128)(2,1)}, f32[2,320]{1,0:T(2,128)S(1)}, f32[2,32,32,320]{3,0,2,1:T(2,128)S(1)}) fusion(f32[2,320]{1,0:T(2,128)S(1)} %copy-done.195, f32[2,320]{1,0:T(2,128)S(1)} %copy-done.172, f32[2,320]{1,0:T(2,128)S(1)} %copy-done.152, ...), kind=kOutput, calls=%fused_computation.222 | convolution fusion | flops 3631675392 | bytes 8414720 | tf_op jit(solution)/shard_map/conv_general_dilated | solution.py:367
  802.4 5.9 fusion.403
  808.4 24.6 %convolution_convert_fusion.1 = bf16[3,3,320,320]{3,2,1,0:T(8,128)(2,1)} fusion(bf16[2,32,32,320]{3,0,2,1:T(2,128)(2,1)S(1)} %get-tuple-element.307, bf16[2,32,32,320]{3,2,1,0:T(8,128)(2,1)S(1)} %bitcast.418), kind=kOutput, calls=%fused_computation.136 | convolution fusion | flops 3620147200 | bytes 4464640 | tf_op jit(solution)/shard_map/conv_general_dilated | solution.py:380
  833.1 24.9 %fusion.441 = f32[2,32,32,320]{3,0,2,1:T(2,128)} fusion(bf16[2,32,32,320]{3,0,2,1:T(2,128)(2,1)S(1)} %get-tuple-element.307, bf16[3,3,320,320]{3,2,1,0:T(8,128)(2,1)S(1)} %copy-done.49), kind=kOutput, calls=%fused_computation.663 | convolution fusion | flops 3619225600 | bytes 5775360 | tf_op jit(solution)/shard_map/conv_general_dilated | solution.py:367
  896.3 2.0 fusion.439
  899.6 2.2 fusion.438
  905.2 5.9 copy.561
  911.1 3.9 multiply_reduce_fusion.16
  918.9 4.0 concatenate.190
  930.1 3.1 concatenate.189.refs_6_
  933.2 96.4 %reduce_all.1 = (f32[360,80]{1,0:T(8,128)}, f32[360,80]{1,0:T(8,128)}, f32[2,40,320]{2,1,0:T(8,128)}, f32[40,640]{1,0:T(8,128)}, f32[160,80]{1,0:T(8,128)}, /*in...) custom-call(s32[8]{0:T(128)} %refs_0_.1, bf16[2,2,2,360,320]{4,3,2,1,0:T(8,128)(2,1)} %bitcast.410, ...), custom_call_target="tpu_custom_call" | custom-call | tf_op jit(solution)/shard_map/reduce_all/pallas_call | solution.py:914
  1047.5 101.2 %soap.1 = (f32[2,320,320]{2,1,0:T(8,128)}, f32[2,2,320,320]{3,2,1,0:T(8,128)}, f32[4,2,40,80]{3,2,1,0:T(8,128)}, f32[8,128]{1,0:T(8,128)}) custom-call(f32[4]{0:T(128)} %pad_maximum_fusion.9.scalars_ref, f32[2,40,320]{2,1,0:T(8,128)} %get-tuple-element.64.part_ref, f32[6,2,320,320]{3,2,1,0:T(8,128)} %state_ref.1), custom_call_target="tpu_custom_call" | custom-call | tf_op jit(solution)/shard_map/soap/pallas_call | solution.py:1171
  1167.2 2.0 multiply_subtract_fusion.1
  (767 shorter events, 221.1 us)
Async XLA Ops:
  7.2 52.2 %copy-start.72 = (f32[2,360,80]{1,2,0:T(8,128)S(1)}, f32[2,360,80]{1,2,0:T(8,128)}, u32[]{:S(2)}) copy-start(f32[2,360,80]{1,2,0:T(8,128)} %param.37) | copy-start | bytes 691204
  7.2 54.9 %copy-start.139 = (f32[96,160]{0,1:T(8,128)S(1)}, f32[96,160]{0,1:T(8,128)}, u32[]{:S(2)}) copy-start(f32[96,160]{0,1:T(8,128)} %param.50) | copy-start | bytes 184324
  7.2 55.6 %copy-start.140 = (f32[96,160]{0,1:T(8,128)S(1)}, f32[96,160]{0,1:T(8,128)}, u32[]{:S(2)}) copy-start(f32[96,160]{0,1:T(8,128)} %param.51) | copy-start | bytes 184324
  7.2 56.3 %copy-start.114 = (f32[96,160]{0,1:T(8,128)S(1)}, f32[96,160]{0,1:T(8,128)}, u32[]{:S(2)}) copy-start(f32[96,160]{0,1:T(8,128)} %param.49) | copy-start | bytes 184324
  7.3 57.1 %copy-start.128 = (bf16[2,1,77,768]{3,0,2,1:T(2,128)(2,1)S(1)}, bf16[2,1,77,768]{3,0,2,1:T(2,128)(2,1)}, u32[]{:S(2)}) copy-start(bf16[2,1,77,768]{3,0,2,1:T(2,128)(2,1)} %param.32) | copy-start | bytes 709636
  7.3 156.1 %all-gather.12.cloned.1.call-start = ((), (), s32[]{:S(2)}) async-start(), calls=%async_computation.1 | async-start | bytes 1689600 | tf_op jit(solution)/shard_map/all_gather | solution.py:1247
  9.0 55.3 %copy-start.125 = (f32[2,360,80]{1,2,0:T(8,128)S(1)}, f32[2,360,80]{1,2,0:T(8,128)}, u32[]{:S(2)}) copy-start(f32[2,360,80]{1,2,0:T(8,128)} %param.38) | copy-start | bytes 691204
  9.0 158.0 %all-gather.10.cloned.1.call-start = ((), (), s32[]{:S(2)}) async-start(), calls=%async_computation | async-start | bytes 5068800 | tf_op jit(solution)/shard_map/all_gather | solution.py:1247
  11.6 53.7 %copy-start.126 = (f32[2,360,80]{1,2,0:T(8,128)S(1)}, f32[2,360,80]{1,2,0:T(8,128)}, u32[]{:S(2)}) copy-start(f32[2,360,80]{1,2,0:T(8,128)} %param.39) | copy-start | bytes 691204
  11.6 204.5 %all-gather.14.cloned.1.call-start = ((), (), s32[]{:S(2)}) async-start(), calls=%async_computation.2 | async-start | bytes 7434240 | tf_op jit(solution)/shard_map/all_gather | solution.py:1247
  64.4 92.0 %copy-start.52 = (bf16[2,1,77,768]{3,2,0,1:T(8,128)(2,1)}, bf16[2,1,77,768]{3,2,0,1:T(8,128)(2,1)S(1)}, u32[]{:S(2)}) copy-start(bf16[2,1,77,768]{3,2,0,1:T(8,128)(2,1)S(1)} %copy.633) | copy-start | bytes 709636
  219.1 54.2 %copy-start.157 = (f32[320]{0:T(512)}, f32[320]{0:T(512)S(1)}, u32[]{:S(2)}) copy-start(f32[320]{0:T(512)S(1)} %get-tuple-element.270) | copy-start | bytes 3844
  219.1 160.8 %copy-start.135 = (f32[320]{0:T(512)}, f32[320]{0:T(512)S(1)}, u32[]{:S(2)}) copy-start(f32[320]{0:T(512)S(1)} %get-tuple-element.271) | copy-start | bytes 3844
  219.8 165.6 %copy-start.159 = (f32[320]{0:T(512)}, f32[320]{0:T(512)S(1)}, u32[]{:S(2)}) copy-start(f32[320]{0:T(512)S(1)} %get-tuple-element.260) | copy-start | bytes 3844
  272.1 107.8 %copy-start.19 = (f32[2,1024,320]{1,2,0:T(8,128)}, f32[2,1024,320]{1,2,0:T(8,128)S(1)}, u32[]{:S(2)}) copy-start(f32[2,1024,320]{1,2,0:T(8,128)S(1)} %get-tuple-element.418) | copy-start | bytes 7864324
  328.7 23.6 %copy-start.151 = (f32[2,320]{1,0:T(2,128)}, f32[2,320]{1,0:T(2,128)S(1)}, u32[]{:S(2)}) copy-start(f32[2,320]{1,0:T(2,128)S(1)} %convolution_add_fusion.3) | copy-start | bytes 7684
  395.6 61.1 %copy-start.15 = (bf16[2,1024,384]{2,1,0:T(8,128)(2,1)}, bf16[2,1024,384]{2,1,0:T(8,128)(2,1)S(1)}, u32[]{:S(2)}) copy-start(bf16[2,1024,384]{2,1,0:T(8,128)(2,1)S(1)} %convolution_convert_fusion.7.q_ref) | copy-start | bytes 4718596
  395.6 61.1 %copy-start.25 = (f32[2,1024,320]{1,2,0:T(8,128)S(1)}, f32[2,1024,320]{1,2,0:T(8,128)}, u32[]{:S(2)}) copy-start(f32[2,1024,320]{1,2,0:T(8,128)} %copy-done.24) | copy-start | bytes 7864324
  395.7 61.1 %copy-start.96 = (bf16[120,320]{0,1:T(8,128)(2,1)S(1)}, bf16[120,320]{0,1:T(8,128)(2,1)}, u32[]{:S(2)}) copy-start(bf16[120,320]{0,1:T(8,128)(2,1)} %copy.520) | copy-start | bytes 230404
  395.7 61.1 %copy-start.98 = (bf16[80,320]{0,1:T(8,128)(2,1)S(1)}, bf16[80,320]{0,1:T(8,128)(2,1)}, u32[]{:S(2)}) copy-start(bf16[80,320]{0,1:T(8,128)(2,1)} %copy.522) | copy-start | bytes 153604
  395.7 61.1 %copy-start.100 = (bf16[120,320]{0,1:T(8,128)(2,1)S(1)}, bf16[120,320]{0,1:T(8,128)(2,1)}, u32[]{:S(2)}) copy-start(bf16[120,320]{0,1:T(8,128)(2,1)} %copy.521) | copy-start | bytes 230404
  395.7 61.1 %copy-start.210 = (f32[320]{0:T(512)S(1)}, f32[320]{0:T(512)}, u32[]{:S(2)}) copy-start(f32[320]{0:T(512)} %get-tuple-element.258) | copy-start | bytes 3844
  457.8 31.8 %copy-start.27 = (f32[2,1024,320]{1,2,0:T(8,128)}, f32[2,1024,320]{1,2,0:T(8,128)S(1)}, u32[]{:S(2)}) copy-start(f32[2,1024,320]{1,2,0:T(8,128)S(1)} %get-tuple-element.424) | copy-start | bytes 7864324
  460.0 29.6 %copy-start.90 = (bf16[120,320]{0,1:T(8,128)(2,1)S(1)}, bf16[120,320]{0,1:T(8,128)(2,1)}, u32[]{:S(2)}) copy-start(bf16[120,320]{0,1:T(8,128)(2,1)} %copy.534) | copy-start | bytes 230404
  460.0 29.6 %copy-start.92 = (bf16[80,320]{0,1:T(8,128)(2,1)S(1)}, bf16[80,320]{0,1:T(8,128)(2,1)}, u32[]{:S(2)}) copy-start(bf16[80,320]{0,1:T(8,128)(2,1)} %copy.536) | copy-start | bytes 153604
  460.0 29.6 %copy-start.94 = (bf16[120,320]{0,1:T(8,128)(2,1)S(1)}, bf16[120,320]{0,1:T(8,128)(2,1)}, u32[]{:S(2)}) copy-start(bf16[120,320]{0,1:T(8,128)(2,1)} %copy.535) | copy-start | bytes 230404
  460.0 29.6 %copy-start.205 = (f32[320]{0:T(512)S(1)}, f32[320]{0:T(512)}, u32[]{:S(2)}) copy-start(f32[320]{0:T(512)} %get-tuple-element.255) | copy-start | bytes 3844
  461.2 29.2 %copy-start.11 = (bf16[2,1024,384]{2,1,0:T(8,128)(2,1)}, bf16[2,1024,384]{2,1,0:T(8,128)(2,1)S(1)}, u32[]{:S(2)}) copy-start(bf16[2,1024,384]{2,1,0:T(8,128)(2,1)S(1)} %convolution_convert_fusion.4.q_ref) | copy-start | bytes 4718596
  490.5 31.7 %copy-start.36 = (f32[2,1024,320]{1,2,0:T(8,128)}, f32[2,1024,320]{1,2,0:T(8,128)S(1)}, u32[]{:S(2)}) copy-start(f32[2,1024,320]{1,2,0:T(8,128)S(1)} %get-tuple-element.426) | copy-start | bytes 7864324
  498.9 23.3 %copy-start.80 = (bf16[1280,320,1]{0,1,2:T(8,128)(2,1)S(1)}, bf16[1280,320,1]{0,1,2:T(8,128)(2,1)}, u32[]{:S(2)}) copy-start(bf16[1280,320,1]{0,1,2:T(8,128)(2,1)} %reshape.874) | copy-start | bytes 2457604
  498.9 23.3 %copy-start.218 = (f32[320]{0:T(512)S(1)}, f32[320]{0:T(512)}, u32[]{:S(2)}) copy-start(f32[320]{0:T(512)} %get-tuple-element.252) | copy-start | bytes 3844
  597.4 30.1 %copy-start.70 = (bf16[2,1024,320]{1,2,0:T(8,128)(2,1)S(1)}, bf16[2,1024,320]{1,2,0:T(8,128)(2,1)}, u32[]{:S(2)}) copy-start(bf16[2,1024,320]{1,2,0:T(8,128)(2,1)} %copy-done.69) | copy-start | bytes 3932164
  639.6 77.7 %copy-start.68 = (bf16[2,1024,320]{1,2,0:T(8,128)(2,1)S(1)}, bf16[2,1024,320]{1,2,0:T(8,128)(2,1)}, u32[]{:S(2)}) copy-start(bf16[2,1024,320]{1,2,0:T(8,128)(2,1)} %copy-done.67) | copy-start | bytes 3932164
  739.8 25.9 %copy-start.35 = (f32[2,32,32,320]{3,0,2,1:T(2,128)S(1)}, f32[2,32,32,320]{3,0,2,1:T(2,128)}, u32[]{:S(2)}) copy-start(f32[2,32,32,320]{3,0,2,1:T(2,128)} %copy-done.34) | copy-start | bytes 7864324
  739.8 25.9 %copy-start.51 = (bf16[3,3,320,320]{3,2,1,0:T(8,128)(2,1)S(1)}, bf16[3,3,320,320]{3,2,1,0:T(8,128)(2,1)}, u32[]{:S(2)}) copy-start(bf16[3,3,320,320]{3,2,1,0:T(8,128)(2,1)} %copy.508) | copy-start | bytes 5529604
  739.8 25.9 %copy-start.61 = (bf16[2,1024,320]{2,1,0:T(8,128)(2,1)S(1)}, bf16[2,1024,320]{2,1,0:T(8,128)(2,1)}, u32[]{:S(2)}) copy-start(bf16[2,1024,320]{2,1,0:T(8,128)(2,1)} %copy.545) | copy-start | bytes 3932164
  739.8 25.9 %copy-start.152 = (f32[2,320]{1,0:T(2,128)S(1)}, f32[2,320]{1,0:T(2,128)}, u32[]{:S(2)}) copy-start(f32[2,320]{1,0:T(2,128)} %copy-done.151) | copy-start | bytes 7684
  739.8 25.9 %copy-start.168 = (f32[320]{0:T(512)S(1)}, f32[320]{0:T(512)}, u32[]{:S(2)}) copy-start(f32[320]{0:T(512)} %get-tuple-element.268) | copy-start | bytes 3844
  739.9 25.9 %copy-start.172 = (f32[2,320]{1,0:T(2,128)S(1)}, f32[2,320]{1,0:T(2,128)}, u32[]{:S(2)}) copy-start(f32[2,320]{1,0:T(2,128)} %copy-done.171) | copy-start | bytes 7684
  739.9 25.9 %copy-start.186 = (f32[320]{0:T(512)S(1)}, f32[320]{0:T(512)}, u32[]{:S(2)}) copy-start(f32[320]{0:T(512)} %get-tuple-element.266) | copy-start | bytes 3844
  739.9 25.9 %copy-start.195 = (f32[2,320]{1,0:T(2,128)S(1)}, f32[2,320]{1,0:T(2,128)}, u32[]{:S(2)}) copy-start(f32[2,320]{1,0:T(2,128)} %copy-done.194) | copy-start | bytes 7684
  739.9 25.9 %copy-start.202 = (f32[320]{0:T(512)S(1)}, f32[320]{0:T(512)}, u32[]{:S(2)}) copy-start(f32[320]{0:T(512)} %get-tuple-element.265) | copy-start | bytes 3844
  765.8 36.0 %copy-start.223 = (s32[320]{0:T(512)S(1)}, s32[320]{0:T(512)}, u32[]{:S(2)}) copy-start(s32[320]{0:T(512)} %add_select_fusion.1) | copy-start | bytes 3844
  808.4 24.6 %copy-start.49 = (bf16[3,3,320,320]{3,2,1,0:T(8,128)(2,1)S(1)}, bf16[3,3,320,320]{3,2,1,0:T(8,128)(2,1)}, u32[]{:S(2)}) copy-start(bf16[3,3,320,320]{3,2,1,0:T(8,128)(2,1)} %copy.503) | copy-start | bytes 5529604
  833.0 25.0 %copy-start.155 = (bf16[2,2880]{1,0:T(2,128)(2,1)S(1)}, bf16[2,2880]{1,0:T(2,128)(2,1)}, u32[]{:S(2)}) copy-start(bf16[2,2880]{1,0:T(2,128)(2,1)} %concatenate.191) | copy-start | bytes 34564
  833.0 25.1 %copy-start.131 = (f32[2,4,1024]{2,1,0:T(4,128)S(1)}, f32[2,4,1024]{2,1,0:T(4,128)}, u32[]{:S(2)}) copy-start(f32[2,4,1024]{2,1,0:T(4,128)} %get-tuple-element.295) | copy-start | bytes 98308
  833.0 25.1 %copy-start.166 = (f32[2,1024]{1,0:T(2,128)S(1)}, f32[2,1024]{1,0:T(2,128)}, u32[]{:S(2)}) copy-start(f32[2,1024]{1,0:T(2,128)} %get-tuple-element.443) | copy-start | bytes 24580
  833.0 26.3 %copy-start.215 = (bf16[4]{0:T(256)(128)(2,1)S(1)}, bf16[4]{0:T(256)(128)(2,1)}, u32[]{:S(2)}) copy-start(bf16[4]{0:T(256)(128)(2,1)} %get-tuple-element.293) | copy-start | bytes 28
  833.0 27.0 %copy-start.227 = (bf16[320]{0:T(512)(128)(2,1)S(1)}, bf16[320]{0:T(512)(128)(2,1)}, u32[]{:S(2)}) copy-start(bf16[320]{0:T(512)(128)(2,1)} %get-tuple-element.229) | copy-start | bytes 1924
  833.0 27.5 %copy-start.226 = (bf16[320]{0:T(512)(128)(2,1)S(1)}, bf16[320]{0:T(512)(128)(2,1)}, u32[]{:S(2)}) copy-start(bf16[320]{0:T(512)(128)(2,1)} %get-tuple-element.238) | copy-start | bytes 1924
  833.0 28.1 %copy-start.211 = (bf16[320]{0:T(512)(128)(2,1)S(1)}, bf16[320]{0:T(512)(128)(2,1)}, u32[]{:S(2)}) copy-start(bf16[320]{0:T(512)(128)(2,1)} %get-tuple-element.296) | copy-start | bytes 1924
  833.1 28.7 %copy-start.176 = (bf16[2560]{0:T(1024)(128)(2,1)S(1)}, bf16[2560]{0:T(1024)(128)(2,1)}, u32[]{:S(2)}) copy-start(bf16[2560]{0:T(1024)(128)(2,1)} %fusion.18) | copy-start | bytes 15364
  833.1 29.4 %copy-start.79 = (bf16[1280,320]{0,1:T(8,128)(2,1)S(1)}, bf16[1280,320]{0,1:T(8,128)(2,1)}, u32[]{:S(2)}) copy-start(bf16[1280,320]{0,1:T(8,128)(2,1)} %fusion.20) | copy-start | bytes 2457604
  833.1 33.4 %copy-start.213 = (bf16[320]{0:T(512)(128)(2,1)S(1)}, bf16[320]{0:T(512)(128)(2,1)}, u32[]{:S(2)}) copy-start(bf16[320]{0:T(512)(128)(2,1)} %get-tuple-element.298) | copy-start | bytes 1924
  833.1 34.0 %copy-start.212 = (bf16[320]{0:T(512)(128)(2,1)S(1)}, bf16[320]{0:T(512)(128)(2,1)}, u32[]{:S(2)}) copy-start(bf16[320]{0:T(512)(128)(2,1)} %get-tuple-element.329) | copy-start | bytes 1924
  863.9 35.7 %copy-start.33 = (bf16[1280,1280]{1,0:T(8,128)(2,1)S(1)}, bf16[1280,1280]{1,0:T(8,128)(2,1)}, u32[]{:S(2)}) copy-start(bf16[1280,1280]{1,0:T(8,128)(2,1)} %reshape.784) | copy-start | bytes 9830404
  863.9 35.7 %copy-start.156 = (f32[2,1280]{1,0:T(2,128)S(1)}, f32[2,1280]{1,0:T(2,128)}, u32[]{:S(2)}) copy-start(f32[2,1280]{1,0:T(2,128)} %get-tuple-element.414) | copy-start | bytes 30724
  1047.4 103.3 %copy-start.106 = (f32[96,160]{1,0:T(8,128)S(1)}, f32[96,160]{1,0:T(8,128)}, u32[]{:S(2)}) copy-start(f32[96,160]{1,0:T(8,128)} %copy.567) | copy-start | bytes 184324
  1047.4 103.3 %copy-start.107 = (f32[96,160]{1,0:T(8,128)S(1)}, f32[96,160]{1,0:T(8,128)}, u32[]{:S(2)}) copy-start(f32[96,160]{1,0:T(8,128)} %copy.568) | copy-start | bytes 184324
  1047.4 103.3 %copy-start.108 = (f32[96,160]{1,0:T(8,128)S(1)}, f32[96,160]{1,0:T(8,128)}, u32[]{:S(2)}) copy-start(f32[96,160]{1,0:T(8,128)} %copy.570) | copy-start | bytes 184324
  1047.5 103.3 %copy-start.109 = (f32[96,160]{1,0:T(8,128)S(1)}, f32[96,160]{1,0:T(8,128)}, u32[]{:S(2)}) copy-start(f32[96,160]{1,0:T(8,128)} %get-tuple-element.61) | copy-start | bytes 184324
  1047.5 104.8 %copy-start.64 = (f32[2,360,80]{2,1,0:T(8,128)S(1)}, f32[2,360,80]{2,1,0:T(8,128)}, u32[]{:S(2)}) copy-start(f32[2,360,80]{2,1,0:T(8,128)} %copy.566) | copy-start | bytes 691204
  1047.5 104.8 %copy-start.65 = (f32[2,360,80]{2,1,0:T(8,128)S(1)}, f32[2,360,80]{2,1,0:T(8,128)}, u32[]{:S(2)}) copy-start(f32[2,360,80]{2,1,0:T(8,128)} %copy.562) | copy-start | bytes 691204
  1047.5 104.8 %copy-start.66 = (f32[2,360,80]{2,1,0:T(8,128)S(1)}, f32[2,360,80]{2,1,0:T(8,128)}, u32[]{:S(2)}) copy-start(f32[2,360,80]{2,1,0:T(8,128)} %copy.564) | copy-start | bytes 691204
  (173 other events, 804.7 us)
Sparse Core Ops, SparseCore 0:
  11.5 57.9 all-gather.11
  72.8 67.9 all-gather.9
  144.2 71.8 all-gather.13
